TPU v7x, 256 devices: a whole 4x4x8 slice. The times are simulated.
256 devices in a mesh: row: 8 (over y, x_hi), theta: 4 (over x_lo, core), gz: 8 (over z).
Axes of the slice: x: 4 (x_hi: 2, x_lo: 2; x = x_hi * 2 + x_lo), y: 4, z: 8, core: 2. Of those that a mesh axis runs over, the one named last changes fastest.
Arguments:
- state_start: float32 [6, 32, 256, 1024], P(None, 'row', 'gz', 'theta'), may hold values from -1.2 to 1.2
- state_section: float32 [6, 32, 256, 1024], P(None, 'row', 'gz', 'theta'), may hold values from -1.5 to 4, as said below
- phase: int32 [32, 256, 1024], P('row', 'gz', 'theta'), may hold values 0 or 1
- cutoff: int32 [4], replicated, may hold values from 1 to 63
Outputs:
- state_next: float32 [6, 32, 256, 1024], P(None, 'row', 'gz', 'theta')
Inputs may be any that keep to these rules, and one draw needn't show every extreme that they name: `state_section`: channel 0 (density) lies in 0.5 to 2.0, channels 1 to 3 (momenta) in -1.5 to 1.5, channel 4 (total energy) in 2.5 to 4.0, channel 5 (jet mass density) in 0 to 1.0.
All inputs are finite; a program needn't handle non-finite values. No bound on the sum of `phase` on one device may be relied on, other than what follows from the above.
Results may differ from a plain program's by a relative error of at most 0.0003.
Values sent between devices are 32-bit elements; how exact they have to be, the bound alone decides.
A program may use at most 64 MiB of HBM per device.

v0:
```python
import math

import jax
import jax.numpy as jnp
from jax import lax
from jax.sharding import PartitionSpec as P

NT = 1024
KMODES = 64


split_speed = 10.0
time_step = 0.05
weno_epsilon = 1e-06
liquid_ratio = 4.4
gas_ratio = 1.4
liquid_stiffness = 0.6


def from_everyone(x, axis):
    copies = jnp.broadcast_to(x, (lax.axis_size(axis), *x.shape))
    return lax.all_to_all(copies, axis, split_axis=0, concat_axis=0, tiled=True)


def of_everyone(x, axis):
    everything = from_everyone(x, axis)
    return jnp.sum(everything, axis=0)


def passed_along(value, axis, steps):
    count = lax.axis_size(axis)
    pairs = [(source, (source + steps) % count) for source in range(count)]
    return lax.ppermute(value, axis, pairs)


def padded_2(x, sides, width):
    edges = {}
    for axis, dim in sides:
        peers, length = (lax.axis_size(axis), x.shape[dim])
        up = [(i, (i + 1) % peers) for i in range(peers)]
        last = lax.slice_in_dim(x, length - width, length, axis=dim)
        first = lax.slice_in_dim(x, 0, width, axis=dim)
        edges[dim] = (
            lax.ppermute(last, axis, up),
            lax.ppermute(first, axis, [(b, a) for a, b in up]),
        )
    done = []
    for _, dim in sides:
        low, high = edges[dim]
        around = [(width, width) if d in done else (0, 0) for d in range(x.ndim)]
        x = jnp.concatenate([jnp.pad(low, around), x, jnp.pad(high, around)], axis=dim)
        done.append(dim)
    return x


def pressure_of(state, phase):
    density = state[0]
    kinetic = 0.5 * (state[1] * state[1] + state[2] * state[2] + state[3] * state[3]) / density
    liquid = phase == 1
    heat_ratio = jnp.where(liquid, liquid_ratio, gas_ratio)
    stiffness = jnp.where(liquid, liquid_stiffness, 0.0)
    return (heat_ratio - 1.0) * (state[4] - kinetic) - heat_ratio * stiffness


def weno_face(far_left, near_left, centre, near_right, far_right):
    smooth_left = (
        13.0 / 12.0 * (far_left - 2.0 * near_left + centre) ** 2
        + 0.25 * (far_left - 4.0 * near_left + 3.0 * centre) ** 2
    )
    smooth_mid = (
        13.0 / 12.0 * (near_left - 2.0 * centre + near_right) ** 2
        + 0.25 * (near_left - near_right) ** 2
    )
    smooth_right = (
        13.0 / 12.0 * (centre - 2.0 * near_right + far_right) ** 2
        + 0.25 * (3.0 * centre - 4.0 * near_right + far_right) ** 2
    )
    weight_left = 0.1 / (weno_epsilon + smooth_left) ** 2
    weight_mid = 0.6 / (weno_epsilon + smooth_mid) ** 2
    weight_right = 0.3 / (weno_epsilon + smooth_right) ** 2
    weight_sum = weight_left + weight_mid + weight_right
    value_left = (2.0 * far_left - 7.0 * near_left + 11.0 * centre) / 6.0
    value_mid = (-near_left + 5.0 * centre + 2.0 * near_right) / 6.0
    value_right = (2.0 * centre + 5.0 * near_right - far_right) / 6.0
    return (
        weight_left * value_left + weight_mid * value_mid + weight_right * value_right
    ) / weight_sum


def face_fluxes(padded_line, array_axis, component):
    density = padded_line[0]
    velocity = padded_line[component] / density
    pressure_field = padded_line[6]
    conserved = padded_line[:6]
    flux_rows = [conserved[channel] * velocity for channel in range(6)]
    flux_rows[component] = flux_rows[component] + pressure_field
    flux_rows[4] = flux_rows[4] + pressure_field * velocity
    physical = jnp.stack(flux_rows)
    upward = 0.5 * (physical + split_speed * conserved)
    downward = 0.5 * (physical - split_speed * conserved)
    face_count = padded_line.shape[array_axis] - 5

    def shifted(values, offset):
        return lax.slice_in_dim(values, offset, offset + face_count, axis=array_axis)

    upwind_part = weno_face(
        shifted(upward, 0),
        shifted(upward, 1),
        shifted(upward, 2),
        shifted(upward, 3),
        shifted(upward, 4),
    )
    downwind_part = weno_face(
        shifted(downward, 5),
        shifted(downward, 4),
        shifted(downward, 3),
        shifted(downward, 2),
        shifted(downward, 1),
    )
    return upwind_part + downwind_part


def tendency(centre_cells, radial_line, axial_line, azimuth_line, cycle_start):
    cycle_count = centre_cells.shape[1]
    radial_flux = face_fluxes(radial_line, 1, 1)
    axial_flux = face_fluxes(axial_line, 2, 3)
    azimuth_flux = face_fluxes(azimuth_line, 3, 2)
    cycle_index = (cycle_start + lax.iota(jnp.int32, cycle_count + 1)).astype(centre_cells.dtype)
    face_radius = cycle_index[None, :, None, None]
    cell_radius = face_radius[:, :-1] + 0.5
    weighted = face_radius * radial_flux
    div_radial = (weighted[:, 1:] - weighted[:, :-1]) / cell_radius
    div_axial = axial_flux[:, :, 1:] - axial_flux[:, :, :-1]
    angle_step = 2.0 * math.pi / NT
    div_azimuth = (azimuth_flux[..., 1:] - azimuth_flux[..., :-1]) / (cell_radius * angle_step)
    density = centre_cells[0]
    swirl_speed = centre_cells[2] / density
    radius = cell_radius[0]
    source_radial = (centre_cells[2] * swirl_speed + centre_cells[6]) / radius
    source_swirl = -centre_cells[1] * swirl_speed / radius
    zero_field = jnp.zeros_like(density)
    source = jnp.stack(
        [zero_field, source_radial, source_swirl, zero_field, zero_field, zero_field]
    )
    return source - div_radial - div_axial - div_azimuth


def across_axis(partner):
    sign_flip = jnp.array([1.0, -1.0, -1.0, 1.0, 1.0, 1.0, 1.0], partner.dtype)[:, None, None, None]
    return partner[:, ::-1] * sign_flip


def build_table(positions, mode_count, length):
    orders = lax.iota(jnp.int32, mode_count)
    phases = positions[:, None] * orders[None, :] % length
    angles = phases.astype(jnp.float32) * (2.0 * math.pi / length)
    return jnp.concatenate([jnp.cos(angles), jnp.sin(angles)], 1)


def cycle_weights(cutoff, mode_count, length):
    orders = lax.iota(jnp.int32, mode_count)
    mode_scale = jnp.where(orders == 0, 1.0 / length, 2.0 / length)
    kept_modes = orders[None, :] <= cutoff[:, None]
    weight_half = jnp.where(kept_modes, mode_scale[None, :], 0.0)
    return jnp.concatenate([weight_half, weight_half], 1)


def apply_filter(cycle_block, weights, theta_id):
    local_theta = cycle_block.shape[3]
    positions = theta_id * local_theta + lax.iota(jnp.int32, local_theta)
    fourier_table = build_table(positions, KMODES, NT)
    coefficients = jnp.einsum(
        "vizt,tk->vizk", cycle_block, fourier_table, precision=lax.Precision.HIGHEST
    )
    coefficients = of_everyone(coefficients, "theta")
    coefficients = coefficients * weights[None, :, None, :]
    return jnp.einsum("vizk,tk->vizt", coefficients, fourier_table, precision=lax.Precision.HIGHEST)


def shards(state_start, state_section, phase, cutoff):
    row_count = lax.axis_size("row")
    row_id = lax.axis_index("row")
    theta_count = lax.axis_size("theta")
    theta_id = lax.axis_index("theta")
    cycle_count = state_section.shape[1]
    filtered_count = cutoff.shape[0]
    pressure_field = pressure_of(state_section, phase)
    fields = jnp.concatenate([state_section, pressure_field[None]], 0)
    partner = passed_along(fields[:, 0:3], "theta", theta_count // 2)
    mirror = across_axis(partner)
    outer_rim = jnp.repeat(fields[:, -1:], 3, axis=1)
    padded = padded_2(fields, (("row", 1), ("theta", 3), ("gz", 2)), 3)
    radial_line = padded[:, :, 3:-3, 3:-3]
    axial_line = padded[:, 3:-3, :, 3:-3]
    azimuth_line = padded[:, 3:-3, 3:-3, :]
    lower_rim = jnp.where(row_id == 0, mirror, radial_line[:, :3])
    upper_rim = jnp.where(row_id == row_count - 1, outer_rim, radial_line[:, -3:])
    radial_line = jnp.concatenate([lower_rim, fields, upper_rim], 1)
    tendencies = tendency(fields, radial_line, axial_line, azimuth_line, row_id * cycle_count)
    advanced = 0.75 * state_start + 0.25 * (state_section + time_step * tendencies)
    weights = cycle_weights(cutoff, KMODES, NT)
    filtered = apply_filter(advanced, weights, theta_id)
    inner_next = jnp.where(row_id == 0, filtered, advanced)
    return jnp.concatenate([inner_next, advanced[:, filtered_count:]], 1)


def solution(mesh):
    in_specs = (
        P(None, "row", "gz", "theta"),
        P(None, "row", "gz", "theta"),
        P("row", "gz", "theta"),
        P(),
    )
    out_specs = P(None, "row", "gz", "theta")
    return jax.shard_map(shards, mesh=mesh, in_specs=in_specs, out_specs=out_specs, check_vma=False)
```

profile of v0, /device:TPU:1, one launch (start us, length us, event | category | flops | bytes accessed | tf_op | source)
XLA Modules:
  0.0 109.0 jit_solution(15044057462193722881)
XLA Ops:
  0.0 1.4 %bitcast_dynamic-update-slice_fusion = (f32[6,4,32,256]{3,2,1,0:T(8,128)S(1)}, f32[4,32,256]{2,1,0:T(8,128)S(1)}) fusion(f32[6,4,32,256]{3,2,1,0:T(8,128)S(1)} %broadcast_dynamic-update-slice_fusion.1, f32[6,4,32,256]{3,2,1,0:T(8,128)} %param.6, f32[4]{0:T(128)S(1)} %get-tuple-element.26, s32[4,32,256]{2,1,0:T(8,128)} %param.7), kind=kLoop, calls=%fused_computation.110 | loop fusion | flops 622592 | bytes 1049088
  1.5 1.1 fusion.13
  2.5 3.2 %collective-permute-start.5 = (f32[7,4,32,3]{3,2,1,0:T(8,128)}, f32[7,4,32,3]{3,2,1,0:T(8,128)}, u32[]{:S(2)}, u32[]{:S(2)}) collective-permute-start(f32[7,4,32,3]{3,2,1,0:T(8,128)} %get-tuple-element.20), channel_id=1, source_target_pairs={{8,0},{16,8},{24,16},{0,24},{9,1},{17,9},{25,17},{1,25},{10,2},{18... | collective-permute-start | bytes 32264 | tf_op jit(solution)/shard_map/ppermute | solution.py:45
  5.7 1.2 %fusion.11 = (f32[7,3,32,256]{3,2,1,0:T(8,128)}, f32[7,3,32,256]{3,2,1,0:T(8,128)}) fusion(f32[6,4,32,256]{3,2,1,0:T(8,128)S(1)} %copy-done, f32[1,4,32,256]{3,2,1,0:T(8,128)S(1)} %bitcast.48), kind=kLoop, calls=%fused_computation.48 | loop fusion | flops 344064 | bytes 2293760 | tf_op jit(solution)/shard_map/concatenate | solution.py:188
  7.0 3.5 %collective-permute-start.2 = (f32[7,3,32,256]{3,2,1,0:T(8,128)}, f32[7,3,32,256]{3,2,1,0:T(8,128)S(1)}, u32[]{:S(2)}, u32[]{:S(2)}) collective-permute-start(f32[7,3,32,256]{3,2,1,0:T(8,128)} %get-tuple-element.22), channel_id=1, source_target_pairs={{32,0},{64,32},{96,64},{128,96},{160,128},{192,160},{224,192},{0,2... | collective-permute-start | bytes 2064392 | tf_op jit(solution)/shard_map/ppermute | solution.py:45
  10.5 0.7 collective-permute-start.4
  11.2 0.7 fusion.48
  11.9 5.6 %collective-permute-start.6 = (f32[7,4,3,256]{3,2,1,0:T(4,128)}, f32[7,4,3,256]{3,2,1,0:T(4,128)}, u32[]{:S(2)}, u32[]{:S(2)}) collective-permute-start(f32[7,4,3,256]{3,2,1,0:T(4,128)} %get-tuple-element.18), channel_id=1, source_target_pairs={{1,0},{2,1},{3,2},{4,3},{5,4},{6,5},{7,6},{0,7},{9,8},{10,9},{11,1... | collective-permute-start | bytes 258056 | tf_op jit(solution)/shard_map/ppermute | solution.py:45
  17.5 0.1 divide_dynamic-update-slice_fusion
  17.6 0.6 fusion.50
  18.2 0.7 fusion.21
  19.0 1.1 %pad.16 = f32[7,10,32,3]{3,2,1,0:T(8,128)S(1)} pad(f32[7,4,32,3]{3,2,1,0:T(8,128)} %collective-permute-done.5, f32[]{:T(128)} %constant.39.clone.1), padding=0_0x3_3x0_0x0_0 | pad | bytes 37636 | tf_op jit(solution)/shard_map/jit(_pad)/pad | solution.py:51
  20.1 26.0 %collective-permute-done.4 = f32[7,4,32,3]{3,2,1,0:T(8,128)} collective-permute-done((f32[7,4,32,3]{3,2,1,0:T(8,128)}, f32[7,4,32,3]{3,2,1,0:T(8,128)}, u32[]{:S(2)}, u32[]{:S(2)}) %collective-permute-start.4) | collective-permute-done | bytes 10784 | tf_op jit(solution)/shard_map/ppermute | solution.py:44
  46.1 1.2 %pad.15 = f32[7,10,32,3]{3,2,1,0:T(8,128)S(1)} pad(f32[7,4,32,3]{3,2,1,0:T(8,128)} %collective-permute-done.4, f32[]{:T(128)} %constant.39.clone.1), padding=0_0x3_3x0_0x0_0 | pad | bytes 37636 | tf_op jit(solution)/shard_map/jit(_pad)/pad | solution.py:51
  47.3 6.7 %select_maximum_fusion = f32[7,10,38,262]{3,2,1,0:T(8,128)S(1)} fusion(f32[7,4,3,256]{3,2,1,0:T(4,128)} %collective-permute-done.6, f32[7,4,3,256]{3,2,1,0:T(4,128)} %collective-permute-done.3, f32[7,10,32,3]{3,2,1,0:T(8,128)S(1)} %pad.16, f32[7,3,32,256]{3,2,1,0:T(8,128)S(1)} %collective-permute-done.2, f32[1,4,32,256]{3,2,1,0:T(8,128)S(1)} %bitcast.51, ...), kind=kLoop, calls=%fused_computation | loop fusion | flops 7666120 | bytes 5307232 | tf_op jit(solution)/shard_map/concatenate | solution.py:51
  54.0 0.2 multiply_dynamic-update-slice_fusion.2
  54.1 0.1 fusion.34
  54.3 0.1 fusion.33
  54.4 0.2 add_dynamic-update-slice_fusion.1
  54.5 0.2 fusion.32
  54.7 0.2 multiply_dynamic-update-slice_fusion.1
  54.9 0.3 fusion.28
  55.2 0.3 fusion.27
  55.5 0.3 fusion.25
  55.7 0.3 fusion.24
  56.1 0.3 fusion.22
  56.4 0.5 add_multiply_fusion.1
  56.9 0.4 copy-done.1
  57.4 0.1 fusion.30
  57.5 0.2 subtract_multiply_fusion.1
  57.7 0.4 add_multiply_fusion.2
  58.1 4.1 %collective-permute-done = f32[7,3,32,256]{3,2,1,0:T(8,128)S(1)} collective-permute-done((f32[7,3,32,256]{3,2,1,0:T(8,128)}, f32[7,3,32,256]{3,2,1,0:T(8,128)S(1)}, u32[]{:S(2)}, u32[]{:S(2)}) %collective-permute-start) | collective-permute-done | bytes 688160 | tf_op jit(solution)/shard_map/ppermute | solution.py:33
  62.2 0.2 multiply_select_fusion
  62.4 0.2 pad_maximum_fusion
  62.5 0.1 multiply_dynamic-update-slice_fusion
  62.9 0.9 add_multiply_fusion
  63.8 5.9 %divide_add_fusion = f32[6,4,32,257]{3,2,1,0:T(8,128)S(1)} fusion(f32[6,4,32,262]{3,2,1,0:T(8,128)S(1)} %subtract_multiply_fusion.1, f32[6,4,32,262]{3,2,1,0:T(8,128)S(1)} %get-tuple-element.11), kind=kLoop, calls=%fused_computation.21 | loop fusion | flops 25461504 | bytes 8684544 | tf_op jit(solution)/shard_map/add | solution.py:120
  69.7 5.0 %divide_add_fusion.1 = f32[6,4,33,256]{3,2,1,0:T(8,128)S(1)} fusion(f32[6,4,38,256]{3,2,1,0:T(8,128)S(1)} %get-tuple-element.14, f32[6,4,38,256]{3,2,1,0:T(8,128)S(1)} %get-tuple-element.13), kind=kLoop, calls=%fused_computation.25 | loop fusion | flops 26155008 | bytes 8921088 | tf_op jit(solution)/shard_map/add | solution.py:120
  74.8 4.7 %add_multiply_fusion.3 = f32[6,5,32,256]{3,2,1,0:T(8,128)S(1)} fusion(f32[6,10,32,256]{3,2,1,0:T(8,128)S(1)} %get-tuple-element.16, f32[6,10,32,256]{3,2,1,0:T(8,128)S(1)} %get-tuple-element.15, f32[5]{0:T(128)S(1)} %add_convert_fusion), kind=kLoop, calls=%fused_computation.28 | loop fusion | flops 31948800 | bytes 10813460 | tf_op jit(solution)/shard_map/mul | solution.py:131
  79.5 0.7 fusion.6
  80.2 0.9 fusion.51
  81.0 1.4 %broadcast_in_dim.54 = f32[4,6,4,32,128]{4,3,2,1,0:T(8,128)} broadcast(f32[6,4,32,128]{3,2,1,0:T(8,128)S(1)} %fusion.51), dimensions={1,2,3,4} | broadcast | bytes 1966080 | tf_op jit(solution)/shard_map/broadcast_in_dim | solution.py:21
  82.4 5.6 %all-to-all-start = ((f32[4,6,4,32,128]{4,3,2,1,0:T(8,128)}), f32[4,6,4,32,128]{4,3,2,1,0:T(8,128)S(1)}, u32[]{:S(2)}, u32[]{:S(2)}) async-start(f32[4,6,4,32,128]{4,3,2,1,0:T(8,128)} %broadcast_in_dim.54), calls=%async_computation | async-start | bytes 3145728 | tf_op jit(solution)/shard_map/all_to_all | solution.py:22
  88.0 0.1 fusion.52
  88.1 0.1 pad_maximum_fusion.10
  88.2 18.9 %all-to-all-done = f32[4,6,4,32,128]{4,3,2,1,0:T(8,128)S(1)} async-done(((f32[4,6,4,32,128]{4,3,2,1,0:T(8,128)}), f32[4,6,4,32,128]{4,3,2,1,0:T(8,128)S(1)}, u32[]{:S(2)}, u32[]{:S(2)}) %all-to-all-start) | async-done | bytes 1572896 | tf_op jit(solution)/shard_map/all_to_all | solution.py:22
  107.1 0.2 reduce_sum.9
  107.3 1.7 %convolution_select_fusion = f32[6,4,32,256]{3,2,1,0:T(8,128)} fusion(f32[6,4,32,256]{3,2,1,0:T(8,128)S(1)} %fusion.6, f32[6,4,32,128]{3,2,1,0:T(8,128)S(1)} %reduce_sum.9, pred[]{:T(512)S(6)} %eq.25, f32[4,128]{1,0:T(4,128)S(1)} %pad_maximum_fusion.10, f32[256,64]{1,0:T(8,128)S(1)} %get-tuple-element.24, f32[256,64]{1,0:T(8,128)S(1)} %get-tuple-element.23), kind=kOutput, calls=%fused_computation.14 | convolution fusion | flops 302317568 | bytes 2099201 | tf_op jit(solution)/shard_map/vizk,tk->vizt/dot_general | solution.py:177
  (31 shorter events, 0.5 us)
Async XLA Ops:
  0.0 1.5 %copy-start = (f32[6,4,32,256]{3,2,1,0:T(8,128)S(1)}, f32[6,4,32,256]{3,2,1,0:T(8,128)}, u32[]{:S(2)}) copy-start(f32[6,4,32,256]{3,2,1,0:T(8,128)} %param.6) | copy-start | bytes 2359300
  2.5 16.4 %collective-permute-start.5 = (f32[7,4,32,3]{3,2,1,0:T(8,128)}, f32[7,4,32,3]{3,2,1,0:T(8,128)}, u32[]{:S(2)}, u32[]{:S(2)}) collective-permute-start(f32[7,4,32,3]{3,2,1,0:T(8,128)} %get-tuple-element.20), channel_id=1, source_target_pairs={{8,0},{16,8},{24,16},{0,24},{9,1},{17,9},{25,17},{1,25},{10,2},{18... | collective-permute-start | bytes 32264 | tf_op jit(solution)/shard_map/ppermute | solution.py:45
  7.0 40.3 %collective-permute-start.2 = (f32[7,3,32,256]{3,2,1,0:T(8,128)}, f32[7,3,32,256]{3,2,1,0:T(8,128)S(1)}, u32[]{:S(2)}, u32[]{:S(2)}) collective-permute-start(f32[7,3,32,256]{3,2,1,0:T(8,128)} %get-tuple-element.22), channel_id=1, source_target_pairs={{32,0},{64,32},{96,64},{128,96},{160,128},{192,160},{224,192},{0,2... | collective-permute-start | bytes 2064392 | tf_op jit(solution)/shard_map/ppermute | solution.py:45
  10.5 36.8 %collective-permute-start.1 = (f32[7,3,32,256]{3,2,1,0:T(8,128)}, f32[7,3,32,256]{3,2,1,0:T(8,128)S(1)}, u32[]{:S(2)}, u32[]{:S(2)}) collective-permute-start(f32[7,3,32,256]{3,2,1,0:T(8,128)} %get-tuple-element.21), channel_id=1, source_target_pairs={{0,32},{32,64},{64,96},{96,128},{128,160},{160,192},{192,224},{224... | collective-permute-start | bytes 2064392 | tf_op jit(solution)/shard_map/ppermute | solution.py:44
  10.5 35.6 %collective-permute-start.4 = (f32[7,4,32,3]{3,2,1,0:T(8,128)}, f32[7,4,32,3]{3,2,1,0:T(8,128)}, u32[]{:S(2)}, u32[]{:S(2)}) collective-permute-start(f32[7,4,32,3]{3,2,1,0:T(8,128)} %get-tuple-element.19), channel_id=1, source_target_pairs={{0,8},{8,16},{16,24},{24,0},{1,9},{9,17},{17,25},{25,1},{2,10},{10... | collective-permute-start | bytes 32264 | tf_op jit(solution)/shard_map/ppermute | solution.py:44
  11.9 35.3 %collective-permute-start.6 = (f32[7,4,3,256]{3,2,1,0:T(4,128)}, f32[7,4,3,256]{3,2,1,0:T(4,128)}, u32[]{:S(2)}, u32[]{:S(2)}) collective-permute-start(f32[7,4,3,256]{3,2,1,0:T(4,128)} %get-tuple-element.18), channel_id=1, source_target_pairs={{1,0},{2,1},{3,2},{4,3},{5,4},{6,5},{7,6},{0,7},{9,8},{10,9},{11,1... | collective-permute-start | bytes 258056 | tf_op jit(solution)/shard_map/ppermute | solution.py:45
  19.0 28.3 %collective-permute-start.3 = (f32[7,4,3,256]{3,2,1,0:T(4,128)S(1)}, f32[7,4,3,256]{3,2,1,0:T(4,128)}, u32[]{:S(2)}, u32[]{:S(2)}) collective-permute-start(f32[7,4,3,256]{3,2,1,0:T(4,128)S(1)} %get-tuple-element.17), channel_id=1, source_target_pairs={{0,1},{1,2},{2,3},{3,4},{4,5},{5,6},{6,7},{7,0},{8,9},{9,10},{10,1... | collective-permute-start | bytes 258056 | tf_op jit(solution)/shard_map/ppermute | solution.py:44
  46.1 16.1 %collective-permute-start = (f32[7,3,32,256]{3,2,1,0:T(8,128)}, f32[7,3,32,256]{3,2,1,0:T(8,128)S(1)}, u32[]{:S(2)}, u32[]{:S(2)}) collective-permute-start(f32[7,3,32,256]{3,2,1,0:T(8,128)} %get-tuple-element.22), channel_id=1, source_target_pairs={{0,16},{8,24},{16,0},{24,8},{1,17},{9,25},{17,1},{25,9},{2,18},{10... | collective-permute-start | bytes 2064392 | tf_op jit(solution)/shard_map/ppermute | solution.py:33
  56.4 0.9 copy-start.1
  57.7 4.5 %copy-start.3 = (f32[7]{0:T(128)S(1)}, f32[7]{0:T(128)}, u32[]{:S(2)}) copy-start(f32[7]{0:T(128)} %constant.69.clone) | copy-start | bytes 88
  74.8 4.7 %copy-start.2 = (f32[6,4,32,256]{3,2,1,0:T(8,128)S(1)}, f32[6,4,32,256]{3,2,1,0:T(8,128)}, u32[]{:S(2)}) copy-start(f32[6,4,32,256]{3,2,1,0:T(8,128)} %param.5) | copy-start | bytes 2359300
  82.4 5.6 %copy-start.4 = (s32[4]{0:T(128)S(1)}, s32[4]{0:T(128)}, u32[]{:S(2)}) copy-start(s32[4]{0:T(128)} %param.8) | copy-start | bytes 52
  82.4 24.7 %all-to-all-start = ((f32[4,6,4,32,128]{4,3,2,1,0:T(8,128)}), f32[4,6,4,32,128]{4,3,2,1,0:T(8,128)S(1)}, u32[]{:S(2)}, u32[]{:S(2)}) async-start(f32[4,6,4,32,128]{4,3,2,1,0:T(8,128)} %broadcast_in_dim.54), calls=%async_computation | async-start | bytes 3145728 | tf_op jit(solution)/shard_map/all_to_all | solution.py:22
where the time goes:
time: 109 us
  waiting for transfers between devices  49 us (45%)
  other arithmetic  34.2 us (31%)
  starting transfers between devices  18.6 us (17%)
  local copies, waits for them, and re-layouts  4.16 us (4%)
  matrix products  2.61 us (2%)
    ppermute x3, waiting for transfers between devices, padded_2(): lax.ppermute(last, axis, up)  26 us
    all_to_all x1, waiting for transfers between devices, from_everyone(): return lax.all_to_all(copies, axis, split_axis=0, concat_axis=0, tiled=True)  18.9 us
    ppermute x3, starting transfers between devices, padded_2(): lax.ppermute(first, axis, [(b, a) for a, b in up])  12.3 us
    add x2, other arithmetic, face_fluxes(): return upwind_part + downwind_part  10.9 us
    concatenate x1, other arithmetic, padded_2(): jnp.concatenate([jnp.pad(low, around), x, jnp.pad(high, around)], axis=dim)  6.69 us
    all_to_all x1, starting transfers between devices, from_everyone(): return lax.all_to_all(copies, axis, split_axis=0, concat_axis=0, tiled=True)  5.59 us
    mul x1, other arithmetic, tendency(): weighted = face_radius * radial_flux  4.7 us
    ppermute x1, waiting for transfers between devices, passed_along(): return lax.ppermute(value, axis, pairs)  4.15 us
  transfers between devices with their start and end apart: 8, of which 3 were waited for; matrix products, arithmetic and copies ran while one was open for 15% of the time, Pallas kernels for 0%

commit v1 on v0

v1 whole, which is shorter than its diff:
```python
import functools
import math

import jax
import jax.numpy as jnp
import numpy as np
from jax import lax
from jax.experimental import pallas as pl
from jax.experimental.pallas import tpu as pltpu
from jax.sharding import PartitionSpec as P

NT = 1024
KMODES = 64
GHOST = 3

split_speed = 10.0
time_step = 0.05
weno_epsilon = 1e-06
scaled_epsilon = 4.0 * weno_epsilon * 12.0 / 13.0
side_scale = 3.0 / 13.0

MESH = pl.DeviceIdType.MESH


def primitives(cells, liquid):
    inverse = 1.0 / cells[0]
    kinetic = 0.5 * (cells[1] * cells[1] + cells[2] * cells[2] + cells[3] * cells[3]) * inverse
    internal = cells[4] - kinetic
    pressure = jnp.where(liquid, 3.4 * internal - 4.4 * 0.6, 0.4 * internal)
    return inverse, pressure


def split_flux(cells, velocity, pressure, component, channel):
    flux = cells[channel] * velocity
    if channel == component:
        flux = flux + pressure
    if channel == 4:
        flux = flux + pressure * velocity
    carried = split_speed * cells[channel]
    return flux + carried, flux - carried


def correction(u1, u2, u3, u4, d0, d1, d2, q0, q1, q2):
    a3 = 3.0 * u2
    b3 = 3.0 * u3
    g0 = a3 - u1
    g1 = u2 + u3
    g2 = u4 - b3
    t0 = q0 + (side_scale * g0) * g0
    t1 = q1 + (side_scale * g1) * g1
    t2 = q2 + (side_scale * g2) * g2
    s0 = t0 * t0
    s1 = t1 * t1
    s2 = t2 * t2
    p0 = s1 * s2
    p1 = (6.0 * s0) * s2
    p2 = (3.0 * s0) * s1
    z0 = d0 + d0 + a3
    z1 = g1 + u3
    z2 = b3 - d2
    top = p0 * z0 + p1 * z1 + p2 * z2
    bottom = p0 + p1 + p2
    return (top / bottom) * (1.0 / 6.0)


def line_divergence(upward, downward, axis):
    length = upward.shape[axis]

    def ahead(x, steps):
        return pltpu.roll(x, (-steps) % length, axis)

    def pieces(field):
        u = ahead(field, 1) - field
        um1 = ahead(u, -1)
        um2 = ahead(u, -2)
        up1 = ahead(u, 1)
        d1 = u - um1
        d0 = um1 - um2
        d2 = up1 - u
        return u, um1, um2, up1, d0, d1, d2, d0 * d0 + scaled_epsilon, d1 * d1 + scaled_epsilon, d2 * d2 + scaled_epsilon

    u, um1, um2, up1, d0, d1, d2, q0, q1, q2 = pieces(upward)
    right = upward + correction(um2, um1, u, up1, d0, d1, d2, q0, q1, q2)
    u, um1, um2, up1, d0, d1, d2, q0, q1, q2 = pieces(downward)
    left = downward - correction(up1, u, um1, um2, -d2, -d1, -d0, q2, q1, q0)
    face = right + ahead(left, 1)
    return face - ahead(face, -1)


def kernel(
    start_hbm,
    section_hbm,
    phase_hbm,
    cutoff_smem,
    table_hbm,
    table_t_hbm,
    out_hbm,
    column,
    column_ph,
    result,
    z_low,
    z_low_ph,
    z_high,
    z_high_ph,
    pack_low,
    pack_high,
    got_low,
    got_high,
    table,
    table_t,
    part,
    half_got,
    half_sum,
    half_far,
    half_total,
    half_peer,
    load_sem,
    load_ph_sem,
    rim_sem,
    misc_sem,
    x_send,
    x_recv,
    y_send,
    y_recv,
    m_send,
    z_send,
    z_recv,
    t_send,
    t_recv,
    f_send,
    f_recv,
    out_sem,
):
    row = lax.axis_index("row")
    theta = lax.axis_index("theta")
    gz = lax.axis_index("gz")
    odd = lax.rem(row, 2)
    partner = row + 1 - 2 * odd
    theta_up = lax.rem(theta + 1, 4)
    theta_down = lax.rem(theta + 3, 4)
    theta_far = lax.rem(theta + 2, 4)
    sibling = theta + 1 - 2 * lax.rem(theta, 2)
    gz_up = lax.rem(gz + 1, 8)
    gz_down = lax.rem(gz + 7, 8)
    first = row == 0
    last = row == 7

    def piece(k):
        octet = k // 2
        half = k % 2
        if isinstance(k, int):
            return pl.ds(octet * 8, 8), pl.ds(half * 128, 128)
        return pl.ds(pl.multiple_of(octet * 8, 8), 8), pl.ds(pl.multiple_of(half * 128, 128), 128)

    def load(k):
        rows, lanes = piece(k)
        return (
            pltpu.make_async_copy(section_hbm.at[:, :, rows, lanes], column.at[:, pl.ds(4, 4), rows, lanes], load_sem.at[k]),
            pltpu.make_async_copy(phase_hbm.at[:, rows, lanes], column_ph.at[pl.ds(4, 4), rows, lanes], load_ph_sem.at[k]),
        )

    for k in range(8):
        for copy in load(k):
            copy.start()
    start_copy = pltpu.make_async_copy(start_hbm, result, misc_sem.at[0])
    start_copy.start()

    def rims():
        copies = []
        for j in range(3):
            copies.append(pltpu.make_async_copy(section_hbm.at[:, pl.ds(3, 1)], column.at[:, pl.ds(8 + j, 1)], rim_sem.at[2 * j]))
            copies.append(pltpu.make_async_copy(phase_hbm.at[pl.ds(3, 1)], column_ph.at[pl.ds(8 + j, 1)], rim_sem.at[2 * j + 1]))
        return copies

    def table_loads():
        return (
            pltpu.make_async_copy(table_hbm.at[pl.ds(pl.multiple_of(theta * 256, 256), 256)], table, misc_sem.at[1]),
            pltpu.make_async_copy(table_t_hbm.at[theta], table_t, misc_sem.at[2]),
        )

    @pl.when(last)
    def _():
        for copy in rims():
            copy.start()

    @pl.when(first)
    def _():
        for copy in table_loads():
            copy.start()

    barrier = pltpu.get_barrier_semaphore()
    for where in (
        {"row": partner},
        {"row": lax.rem(row + 2, 8)},
        {"row": lax.rem(row + 6, 8)},
        {"theta": theta_up},
        {"theta": theta_down},
        {"theta": theta_far},
        {"gz": gz_up},
        {"gz": gz_down},
    ):
        pl.semaphore_signal(barrier, inc=1, device_id=where, device_id_type=MESH)
    pl.semaphore_wait(barrier, 8)

    def carry(k, source, target, count, send, recv, where):
        rows, lanes = piece(k)
        return (
            pltpu.make_async_remote_copy(
                src_ref=column.at[:, pl.ds(source, count), rows, lanes],
                dst_ref=column.at[:, pl.ds(target, count), rows, lanes],
                send_sem=send.at[k],
                recv_sem=recv.at[k],
                device_id=where,
                device_id_type=MESH,
            ),
            pltpu.make_async_remote_copy(
                src_ref=column_ph.at[pl.ds(source, count), rows, lanes],
                dst_ref=column_ph.at[pl.ds(target, count), rows, lanes],
                send_sem=send.at[k + 8],
                recv_sem=recv.at[k + 8],
                device_id=where,
                device_id_type=MESH,
            ),
        )

    inner_row = jnp.logical_and(row > 0, row < 7)
    to_partner = {"row": partner}

    def x_full(k):
        return carry(k, 4, 8 * odd, 4, x_send, x_recv, to_partner)

    def x_first(k):
        return carry(k, 5, 1, 3, x_send, x_recv, to_partner)

    def x_last(k):
        return carry(k, 4, 8, 3, x_send, x_recv, to_partner)

    def mirror(k):
        return carry(k, 4, 1, 3, m_send, y_recv, {"theta": theta_far})

    def forward(k):
        target = jnp.where(odd == 1, lax.rem(row + 6, 8), lax.rem(row + 2, 8))
        return carry(k, 9 - 9 * odd, 1 + 7 * odd, 3, y_send, y_recv, {"row": target})

    forwards = jnp.logical_or(jnp.logical_and(odd == 0, row < 6), jnp.logical_and(odd == 1, row > 1))

    def z_copies():
        copies = []
        for side, (rows, cells_to, phase_to, where) in enumerate(
            (
                (pl.ds(0, 8), z_high, z_high_ph, {"gz": gz_down}),
                (pl.ds(24, 8), z_low, z_low_ph, {"gz": gz_up}),
            )
        ):
            copies.append(
                pltpu.make_async_remote_copy(
                    src_ref=column.at[:, pl.ds(4, 4), rows, :],
                    dst_ref=cells_to,
                    send_sem=z_send.at[2 * side],
                    recv_sem=z_recv.at[2 * side],
                    device_id=where,
                    device_id_type=MESH,
                )
            )
            copies.append(
                pltpu.make_async_remote_copy(
                    src_ref=column_ph.at[pl.ds(4, 4), rows, :],
                    dst_ref=phase_to,
                    send_sem=z_send.at[2 * side + 1],
                    recv_sem=z_recv.at[2 * side + 1],
                    device_id=where,
                    device_id_type=MESH,
                )
            )
        return copies

    for k in range(8):
        for copy in load(k):
            copy.wait()

        @pl.when(inner_row)
        def _():
            for copy in x_full(k):
                copy.start()

        @pl.when(first)
        def _():
            for copy in x_first(k):
                copy.start()
            for copy in mirror(k):
                copy.start()

        @pl.when(last)
        def _():
            for copy in x_last(k):
                copy.start()

    for copy in z_copies():
        copy.start()

    lane = lax.broadcasted_iota(jnp.int32, (8, 128), 1)

    def pack(n, _):
        pair = n // 4
        rows = pl.ds(pl.multiple_of((n % 4) * 8, 8), 8)
        low = jnp.zeros((8, 128), jnp.float32)
        high = jnp.zeros((8, 128), jnp.float32)
        for group in range(14):
            channel, cycle = group % 7, 4 + 2 * pair + group // 7
            if channel < 6:
                near = column[channel, cycle, rows, pl.ds(0, 128)]
                far = column[channel, cycle, rows, pl.ds(128, 128)]
            else:
                near = column_ph[cycle, rows, pl.ds(0, 128)].astype(jnp.float32)
                far = column_ph[cycle, rows, pl.ds(128, 128)].astype(jnp.float32)
            if group:
                near = pltpu.roll(near, 8 * group, 1)
            far = pltpu.roll(far, (8 * group + 8) % 128, 1)
            here = lane // 8 == group
            low = jnp.where(here, near, low)
            high = jnp.where(here, far, high)
        pack_low[pair, rows, :] = low
        pack_high[pair, rows, :] = high
        return 0

    lax.fori_loop(0, 8, pack, 0)

    def t_copies():
        return (
            pltpu.make_async_remote_copy(
                src_ref=pack_low,
                dst_ref=got_high,
                send_sem=t_send.at[0],
                recv_sem=t_recv.at[0],
                device_id={"theta": theta_down},
                device_id_type=MESH,
            ),
            pltpu.make_async_remote_copy(
                src_ref=pack_high,
                dst_ref=got_low,
                send_sem=t_send.at[1],
                recv_sem=t_recv.at[1],
                device_id={"theta": theta_up},
                device_id_type=MESH,
            ),
        )

    for copy in t_copies():
        copy.start()
    start_copy.wait()
    for copy in t_copies():
        copy.wait_recv()

    quarter = 0.25 * time_step

    def azimuthal(n, _):
        cycle = n // 4
        octet = n % 4
        rows = pl.ds(pl.multiple_of(octet * 8, 8), 8)
        pair = cycle // 2
        low = got_low[pair, rows, :]
        high = got_high[pair, rows, :]
        base = lax.rem(cycle, 2) * 56

        def edge(channel):
            offset = base + 8 * channel
            upper = pltpu.roll(high, lax.rem(128 - offset, 128), 1)
            lower = pltpu.roll(low, 120 - offset, 1)
            return jnp.where(lane < 64, upper, lower)

        cells = [jnp.concatenate([column[c, 4 + cycle, rows, :], edge(c)], 1) for c in range(6)]
        material = jnp.concatenate([column_ph[4 + cycle, rows, :].astype(jnp.float32), edge(6)], 1)
        inverse, pressure = primitives(cells, material > 0.5)
        velocity = cells[2] * inverse
        radius = (row * 4 + cycle).astype(jnp.float32) + 0.5
        scale = 0.5 * quarter / (radius * (2.0 * math.pi / NT))
        source_scale = quarter / radius
        for c in range(6):
            upward, downward = split_flux(cells, velocity, pressure, 2, c)
            change = line_divergence(upward, downward, 1)[:, :256] * scale
            value = 0.75 * result[c, cycle, rows, :] + 0.25 * cells[c][:, :256] - change
            if c == 1:
                value = value + source_scale * (cells[2] * velocity + pressure)[:, :256]
            if c == 2:
                value = value - source_scale * (cells[1] * velocity)[:, :256]
            result[c, cycle, rows, :] = value
        return 0

    lax.fori_loop(0, 16, azimuthal, 0)

    row8 = lax.broadcasted_iota(jnp.int32, (8, 128), 0)

    def axial(n):
        cycle = n // 2
        lanes = pl.ds(pl.multiple_of((n % 2) * 128, 128), 128)
        cells = [
            jnp.concatenate(
                [column[c, 4 + cycle, :, lanes], jnp.where(row8 < 4, z_high[c, cycle, :, lanes], z_low[c, cycle, :, lanes])], 0
            )
            for c in range(6)
        ]
        material = jnp.concatenate(
            [column_ph[4 + cycle, :, lanes], jnp.where(row8 < 4, z_high_ph[cycle, :, lanes], z_low_ph[cycle, :, lanes])], 0
        )
        inverse, pressure = primitives(cells, material == 1)
        velocity = cells[3] * inverse
        for c in range(6):
            upward, downward = split_flux(cells, velocity, pressure, 3, c)
            change = line_divergence(upward, downward, 0)[:32] * (0.5 * quarter)
            result[c, cycle, :, lanes] = result[c, cycle, :, lanes] - change

    def arrive_and_forward(k):
        @pl.when(jnp.logical_and(row != 1, row != 6))
        def _():
            for copy in carry(k, 4, 4, 4, x_send, x_recv, to_partner):
                copy.wait_recv()

        @pl.when(jnp.logical_or(row == 1, row == 6))
        def _():
            for copy in carry(k, 4, 4, 3, x_send, x_recv, to_partner):
                copy.wait_recv()

        @pl.when(forwards)
        def _():
            for copy in forward(k):
                copy.start()

    def y_arrive(k):
        @pl.when(row != 7)
        def _():
            for copy in carry(k, 4, 4, 3, y_send, y_recv, to_partner):
                copy.wait_recv()

    flip = jnp.where(first, -1.0, 1.0)

    def radial(k):
        rows, lanes = piece(k)
        planes = [jnp.where(first, 4 - p, p) for p in (1, 2, 3)] + list(range(4, 11))
        stack = []
        for i, plane in enumerate(planes):
            cells = [column[c, plane, rows, lanes] for c in range(6)]
            if i < 3:
                cells[1] = cells[1] * flip
                cells[2] = cells[2] * flip
            inverse, pressure = primitives(cells, column_ph[plane, rows, lanes] == 1)
            stack.append((cells, cells[1] * inverse, pressure))
        for c in range(6):
            up, down = zip(*[split_flux(cells, v, p, 1, c) for cells, v, p in stack])

            def pieces(field):
                u = [field[i + 1] - field[i] for i in range(9)]
                d = [None] + [u[i] - u[i - 1] for i in range(1, 9)]
                q = [None] + [d[i] * d[i] + scaled_epsilon for i in range(1, 9)]
                return u, d, q

            u, d, q = pieces(up)
            right = [
                up[i] + correction(u[i - 2], u[i - 1], u[i], u[i + 1], d[i - 1], d[i], d[i + 1], q[i - 1], q[i], q[i + 1])
                for i in range(2, 7)
            ]
            u, d, q = pieces(down)
            left = [
                down[i] - correction(u[i + 1], u[i], u[i - 1], u[i - 2], -d[i + 1], -d[i], -d[i - 1], q[i + 1], q[i], q[i - 1])
                for i in range(3, 8)
            ]
            face = [a + b for a, b in zip(right, left)]
            weighted = [(row * 4 + j).astype(jnp.float32) * face[j] for j in range(5)]
            for j in range(4):
                radius = (row * 4 + j).astype(jnp.float32) + 0.5
                result[c, j, rows, lanes] = result[c, j, rows, lanes] - (weighted[j + 1] - weighted[j]) * (0.5 * quarter / radius)

    for copy in z_copies():
        copy.wait_recv()
    arrive_and_forward(0)

    def axial_pair(n, _):
        axial(2 * n)
        axial(2 * n + 1)
        arrive_and_forward(n + 1)
        return 0

    lax.fori_loop(0, 4, axial_pair, 0)

    @pl.when(last)
    def _():
        for copy in rims():
            copy.wait()

    def radial_step(k, _):
        @pl.when(k + 5 < 8)
        def _():
            arrive_and_forward(k + 5)

        y_arrive(k)
        radial(k)
        return 0

    lax.fori_loop(0, 8, radial_step, 0)

    def out_copy(o):
        rows = pl.ds(o * 8, 8)
        return pltpu.make_async_copy(result.at[:, :, rows, :], out_hbm.at[:, :, rows, :], out_sem.at[o])

    @pl.when(first)
    def _():
        for copy in table_loads():
            copy.wait()
        mine = lax.rem(theta, 2) * 96
        other = 96 - mine
        pairs = ((0, {"theta": sibling}), (4, {"theta": theta_far}), (8, {"theta": sibling}))

        def share(step, o, source, target):
            base, where = pairs[step]
            return pltpu.make_async_remote_copy(
                src_ref=source,
                dst_ref=target,
                send_sem=f_send.at[base + o],
                recv_sem=f_recv.at[base + o],
                device_id=where,
                device_id_type=MESH,
            )

        def step_one(o):
            return share(0, o, part.at[o, pl.ds(pl.multiple_of(other, 8), 96)], half_got.at[o])

        def step_two(o):
            return share(1, o, half_sum.at[o], half_far.at[o])

        def step_three(o):
            return share(2, o, half_total.at[o], half_peer.at[o])

        for o in range(4):
            values = result[:, :, pl.ds(8 * o, 8), :].reshape(192, 256)
            part[o] = jnp.dot(values, table[...], precision=lax.Precision.HIGHEST, preferred_element_type=jnp.float32)
            step_one(o).start()
        for o in range(4):
            step_one(o).wait_recv()
            half_sum[o] = part[o, pl.ds(pl.multiple_of(mine, 8), 96)] + half_got[o]
            step_two(o).start()
        for o in range(4):
            step_two(o).wait_recv()
            half_total[o] = half_sum[o] + half_far[o]
            step_three(o).start()
        order = lax.broadcasted_iota(jnp.int32, (8, 128), 1)
        order = jnp.where(order < KMODES, order, order - KMODES)
        mode_scale = jnp.where(order == 0, 1.0 / NT, 2.0 / NT)
        weights = [jnp.where(order <= cutoff_smem[i], mode_scale, 0.0) for i in range(4)]
        weights = jnp.concatenate(weights * 3, 0)
        even_core = mine == 0
        for o in range(4):
            step_three(o).wait_recv()
            own = half_total[o] * weights
            peer = half_peer[o] * weights
            lower = jnp.where(even_core, own, peer)
            upper = jnp.where(even_core, peer, own)
            coefficients = jnp.concatenate([lower, upper], 0)
            values = jnp.dot(coefficients, table_t[...], precision=lax.Precision.HIGHEST, preferred_element_type=jnp.float32)
            result[:, :, pl.ds(8 * o, 8), :] = values.reshape(6, 4, 8, 256)
            out_copy(o).start()
        for o in range(4):
            step_one(o).wait_send()
            step_two(o).wait_send()
            step_three(o).wait_send()

    @pl.when(jnp.logical_not(first))
    def _():
        for o in range(4):
            out_copy(o).start()

    for copy in t_copies():
        copy.wait_send()
    for copy in z_copies():
        copy.wait_send()
    for k in range(8):

        @pl.when(inner_row)
        def _():
            for copy in x_full(k):
                copy.wait_send()

        @pl.when(jnp.logical_not(inner_row))
        def _():
            for copy in x_last(k):
                copy.wait_send()

        @pl.when(first)
        def _():
            for copy in mirror(k):
                copy.wait_send()

        @pl.when(forwards)
        def _():
            for copy in forward(k):
                copy.wait_send()

    for o in range(4):
        out_copy(o).wait()


def fourier_tables():
    phases = (np.arange(NT)[:, None] * np.arange(KMODES)[None, :]) % NT
    angles = phases.astype(np.float64) * (2.0 * np.pi / NT)
    table = np.concatenate([np.cos(angles), np.sin(angles)], 1).astype(np.float32)
    return table, np.ascontiguousarray(table.reshape(4, 256, 2 * KMODES).transpose(0, 2, 1))


def shards(state_start, state_section, phase, cutoff):
    f32, i32 = jnp.float32, jnp.int32
    table, table_t = fourier_tables()
    anywhere = pl.BlockSpec(memory_space=pl.ANY)
    dma = pltpu.SemaphoreType.DMA
    return pl.pallas_call(
        kernel,
        out_shape=jax.ShapeDtypeStruct(state_start.shape, f32),
        in_specs=[anywhere, anywhere, anywhere, pl.BlockSpec(memory_space=pltpu.SMEM), anywhere, anywhere],
        out_specs=anywhere,
        scratch_shapes=[
            pltpu.VMEM((6, 12, 32, 256), f32),
            pltpu.VMEM((12, 32, 256), i32),
            pltpu.VMEM((6, 4, 32, 256), f32),
            pltpu.VMEM((6, 4, 8, 256), f32),
            pltpu.VMEM((4, 8, 256), i32),
            pltpu.VMEM((6, 4, 8, 256), f32),
            pltpu.VMEM((4, 8, 256), i32),
            pltpu.VMEM((2, 32, 128), f32),
            pltpu.VMEM((2, 32, 128), f32),
            pltpu.VMEM((2, 32, 128), f32),
            pltpu.VMEM((2, 32, 128), f32),
            pltpu.VMEM((256, 2 * KMODES), f32),
            pltpu.VMEM((2 * KMODES, 256), f32),
            pltpu.VMEM((4, 192, 2 * KMODES), f32),
            pltpu.VMEM((4, 96, 2 * KMODES), f32),
            pltpu.VMEM((4, 96, 2 * KMODES), f32),
            pltpu.VMEM((4, 96, 2 * KMODES), f32),
            pltpu.VMEM((4, 96, 2 * KMODES), f32),
            pltpu.VMEM((4, 96, 2 * KMODES), f32),
            dma((8,)),
            dma((8,)),
            dma((6,)),
            dma((3,)),
            dma((16,)),
            dma((16,)),
            dma((16,)),
            dma((16,)),
            dma((16,)),
            dma((4,)),
            dma((4,)),
            dma((2,)),
            dma((2,)),
            dma((12,)),
            dma((12,)),
            dma((4,)),
        ],
        compiler_params=pltpu.CompilerParams(collective_id=0, has_side_effects=True, vmem_limit_bytes=40 * 1024 * 1024),
        name="jet_section",
    )(state_start, state_section, phase, cutoff, jnp.asarray(table), jnp.asarray(table_t))


def solution(mesh):
    in_specs = (
        P(None, "row", "gz", "theta"),
        P(None, "row", "gz", "theta"),
        P("row", "gz", "theta"),
        P(),
    )
    out_specs = P(None, "row", "gz", "theta")
    return jax.shard_map(shards, mesh=mesh, in_specs=in_specs, out_specs=out_specs, check_vma=False)
```

time: 109 us -> 75.7 us (0.69)
  Pallas kernels: 0 us -> 68.6 us
  waiting for transfers between devices: 49 us -> 0 us
  other arithmetic: 34.2 us -> 0 us
  starting transfers between devices: 18.6 us -> 0 us
  local copies, waits for them, and re-layouts: 4.16 us -> 6.79 us
  matrix products: 2.61 us -> 0 us
    pallas_call x0 -> x1, Pallas kernels: none -> 68.6 us  [shards(): pl.pallas_call(kernel, out_shape=jax.ShapeDtypeStruct(state_start.shape,...]
    ppermute x7 -> x0, waiting for transfers between devices: 30.1 us -> none  [the longest x3 26 us: padded_2(): lax.ppermute(last, axis, up)]
    all_to_all x1 -> x0, waiting for transfers between devices: 18.9 us -> none  [from_everyone(): return lax.all_to_all(copies, axis, split_axis=0, concat_axis=0, tiled=True)]
    ppermute x7 -> x0, starting transfers between devices: 13 us -> none  [the longest x3 12.3 us: padded_2(): lax.ppermute(first, axis, [(b, a) for a, b in up])]
    add x4 -> x0, other arithmetic: 11.6 us -> none  [the longest x2 10.9 us: face_fluxes(): return upwind_part + downwind_part]
    concatenate x6 -> x0, other arithmetic: 9.94 us -> none  [the longest x1 6.69 us: padded_2(): jnp.concatenate([jnp.pad(low, around), x, jnp.pad(high, around)], axis=dim)]
    mul x5 -> x0, other arithmetic: 6.67 us -> none  [the longest x1 4.7 us: tendency(): weighted = face_radius * radial_flux]
    unnamed x12 -> x13, local copies, waits for them, and re-layouts: 0.48 us -> 6.79 us
  transfers between devices with their start and end apart: 8 -> 0, of which waited for: 3 -> 0; matrix products, arithmetic and copies ran while one was open for 15% -> 0% of each run, Pallas kernels for 0% -> 0%
where the time goes in v1:
time: 75.7 us; the launch traced here: 75.4 us
  Pallas kernels  68.6 us (91%)
  local copies, waits for them, and re-layouts  6.79 us (9%)
    pallas_call x1, Pallas kernels, shards(): pl.pallas_call(kernel, out_shape=jax.ShapeDtypeStruct(state_start.shape,...  68.6 us
    unnamed x13, local copies, waits for them, and re-layouts  6.79 us

profile of v1, /device:TPU:1, one launch (start us, length us, event | category | flops | bytes accessed | tf_op | source)
XLA Modules:
  0.0 75.4 jit_solution(4690942531184284189)
XLA Ops:
  0.0 0.0 copy-start
  0.0 1.1 %copy-done = f32[6,4,32,256]{3,2,1,0:T(8,128)S(1)} copy-done((f32[6,4,32,256]{3,2,1,0:T(8,128)S(1)}, f32[6,4,32,256]{3,2,1,0:T(8,128)}, u32[]{:S(2)}) %copy-start) | copy-done | bytes 786456
  1.1 0.0 copy-start.1
  1.1 1.1 %copy-done.1 = f32[6,4,32,256]{3,2,1,0:T(8,128)S(1)} copy-done((f32[6,4,32,256]{3,2,1,0:T(8,128)S(1)}, f32[6,4,32,256]{3,2,1,0:T(8,128)}, u32[]{:S(2)}) %copy-start.1) | copy-done | bytes 786456
  2.3 0.0 copy-start.2
  2.3 1.0 %copy-done.2 = f32[4,128,256]{2,1,0:T(8,128)S(1)} copy-done((f32[4,128,256]{2,1,0:T(8,128)S(1)}, f32[4,128,256]{2,1,0:T(8,128)}, u32[]{:S(2)}) %copy-start.2) | copy-done | bytes 524312
  3.3 0.0 copy-start.3
  3.3 1.0 %copy-done.3 = f32[1024,128]{1,0:T(8,128)S(1)} copy-done((f32[1024,128]{1,0:T(8,128)S(1)}, f32[1024,128]{1,0:T(8,128)}, u32[]{:S(2)}) %copy-start.3) | copy-done | bytes 524312
  4.4 0.0 copy-start.4
  4.4 0.9 %copy-done.4 = s32[4,32,256]{2,1,0:T(8,128)S(1)} copy-done((s32[4,32,256]{2,1,0:T(8,128)S(1)}, s32[4,32,256]{2,1,0:T(8,128)}, u32[]{:S(2)}) %copy-start.4) | copy-done | bytes 131096
  5.3 0.0 copy-start.5
  5.3 0.7 copy-done.5
  5.9 68.6 %jet_section.1 = f32[6,4,32,256]{3,2,1,0:T(8,128)S(1)} custom-call(f32[6,4,32,256]{3,2,1,0:T(8,128)S(1)} %copy-done, f32[6,4,32,256]{3,2,1,0:T(8,128)S(1)} %copy-done.1, s32[4,32,256]{2,1,0:T(8,128)S(1)} %copy-done.4, s32[4]{0:T(128)S(1)} %copy-done.5, f32[1024,128]{1,0:T(8,128)S(1)} %copy-done.3, f32[4,128,256]{2,1,0:T(8,128)S(1)} %copy-done.2), custom_call_target="tpu_custom_call" | custom-call | tf_op jit(solution)/shard_map/jet_section/pallas_call | solution.py:612
  74.6 0.9 %copy.8 = f32[6,4,32,256]{3,2,1,0:T(8,128)} copy(f32[6,4,32,256]{3,2,1,0:T(8,128)S(1)} %jet_section.1) | data formatting | bytes 1572864
Async XLA Ops:
  0.0 1.1 %copy-start = (f32[6,4,32,256]{3,2,1,0:T(8,128)S(1)}, f32[6,4,32,256]{3,2,1,0:T(8,128)}, u32[]{:S(2)}) copy-start(f32[6,4,32,256]{3,2,1,0:T(8,128)} %start_hbm.1) | copy-start | bytes 2359300
  1.1 1.1 %copy-start.1 = (f32[6,4,32,256]{3,2,1,0:T(8,128)S(1)}, f32[6,4,32,256]{3,2,1,0:T(8,128)}, u32[]{:S(2)}) copy-start(f32[6,4,32,256]{3,2,1,0:T(8,128)} %section_hbm.1) | copy-start | bytes 2359300
  2.3 1.0 %copy-start.2 = (f32[4,128,256]{2,1,0:T(8,128)S(1)}, f32[4,128,256]{2,1,0:T(8,128)}, u32[]{:S(2)}) copy-start(f32[4,128,256]{2,1,0:T(8,128)} %constant.5.clone.table_t_hbm) | copy-start | bytes 1572868
  3.3 1.0 %copy-start.3 = (f32[1024,128]{1,0:T(8,128)S(1)}, f32[1024,128]{1,0:T(8,128)}, u32[]{:S(2)}) copy-start(f32[1024,128]{1,0:T(8,128)} %constant.4.clone.table_hbm) | copy-start | bytes 1572868
  4.4 0.9 %copy-start.4 = (s32[4,32,256]{2,1,0:T(8,128)S(1)}, s32[4,32,256]{2,1,0:T(8,128)}, u32[]{:S(2)}) copy-start(s32[4,32,256]{2,1,0:T(8,128)} %phase_hbm.1) | copy-start | bytes 393220
  5.3 0.7 copy-start.5

commit v2 on v1

--- a/solution.py
+++ b/solution.py
@@ -91,7 +91,7 @@
     start_hbm,
     section_hbm,
     phase_hbm,
-    cutoff_smem,
+    cutoff_hbm,
     table_hbm,
     table_t_hbm,
     out_hbm,
@@ -114,6 +114,7 @@
     half_far,
     half_total,
     half_peer,
+    cutoff_smem,
     load_sem,
     load_ph_sem,
     rim_sem,
@@ -176,6 +177,7 @@
         return (
             pltpu.make_async_copy(table_hbm.at[pl.ds(pl.multiple_of(theta * 256, 256), 256)], table, misc_sem.at[1]),
             pltpu.make_async_copy(table_t_hbm.at[theta], table_t, misc_sem.at[2]),
+            pltpu.make_async_copy(cutoff_hbm, cutoff_smem, misc_sem.at[3]),
         )
 
     @pl.when(last)
@@ -200,7 +202,6 @@
         {"gz": gz_down},
     ):
         pl.semaphore_signal(barrier, inc=1, device_id=where, device_id_type=MESH)
-    pl.semaphore_wait(barrier, 8)
 
     def carry(k, source, target, count, send, recv, where):
         rows, lanes = piece(k)
@@ -222,6 +223,37 @@
                 device_id_type=MESH,
             ),
         )
+
+    for k in range(8):
+        for copy in load(k):
+            copy.wait()
+
+    lane = lax.broadcasted_iota(jnp.int32, (8, 128), 1)
+
+    def pack(n, _):
+        pair = n // 4
+        rows = pl.ds(pl.multiple_of((n % 4) * 8, 8), 8)
+        low = jnp.zeros((8, 128), jnp.float32)
+        high = jnp.zeros((8, 128), jnp.float32)
+        for group in range(14):
+            channel, cycle = group % 7, 4 + 2 * pair + group // 7
+            if channel < 6:
+                near = column[channel, cycle, rows, pl.ds(0, 128)]
+                far = column[channel, cycle, rows, pl.ds(128, 128)]
+            else:
+                near = column_ph[cycle, rows, pl.ds(0, 128)].astype(jnp.float32)
+                far = column_ph[cycle, rows, pl.ds(128, 128)].astype(jnp.float32)
+            if group:
+                near = pltpu.roll(near, 8 * group, 1)
+            far = pltpu.roll(far, (8 * group + 8) % 128, 1)
+            here = lane // 8 == group
+            low = jnp.where(here, near, low)
+            high = jnp.where(here, far, high)
+        pack_low[pair, rows, :] = low
+        pack_high[pair, rows, :] = high
+        return 0
+
+    lax.fori_loop(0, 8, pack, 0)
 
     inner_row = jnp.logical_and(row > 0, row < 7)
     to_partner = {"row": partner}
@@ -274,57 +306,6 @@
             )
         return copies
 
-    for k in range(8):
-        for copy in load(k):
-            copy.wait()
-
-        @pl.when(inner_row)
-        def _():
-            for copy in x_full(k):
-                copy.start()
-
-        @pl.when(first)
-        def _():
-            for copy in x_first(k):
-                copy.start()
-            for copy in mirror(k):
-                copy.start()
-
-        @pl.when(last)
-        def _():
-            for copy in x_last(k):
-                copy.start()
-
-    for copy in z_copies():
-        copy.start()
-
-    lane = lax.broadcasted_iota(jnp.int32, (8, 128), 1)
-
-    def pack(n, _):
-        pair = n // 4
-        rows = pl.ds(pl.multiple_of((n % 4) * 8, 8), 8)
-        low = jnp.zeros((8, 128), jnp.float32)
-        high = jnp.zeros((8, 128), jnp.float32)
-        for group in range(14):
-            channel, cycle = group % 7, 4 + 2 * pair + group // 7
-            if channel < 6:
-                near = column[channel, cycle, rows, pl.ds(0, 128)]
-                far = column[channel, cycle, rows, pl.ds(128, 128)]
-            else:
-                near = column_ph[cycle, rows, pl.ds(0, 128)].astype(jnp.float32)
-                far = column_ph[cycle, rows, pl.ds(128, 128)].astype(jnp.float32)
-            if group:
-                near = pltpu.roll(near, 8 * group, 1)
-            far = pltpu.roll(far, (8 * group + 8) % 128, 1)
-            here = lane // 8 == group
-            low = jnp.where(here, near, low)
-            high = jnp.where(here, far, high)
-        pack_low[pair, rows, :] = low
-        pack_high[pair, rows, :] = high
-        return 0
-
-    lax.fori_loop(0, 8, pack, 0)
-
     def t_copies():
         return (
             pltpu.make_async_remote_copy(
@@ -345,8 +326,31 @@
             ),
         )
 
+    pl.semaphore_wait(barrier, 8)
     for copy in t_copies():
         copy.start()
+    for copy in z_copies():
+        copy.start()
+
+    for k in range(8):
+
+        @pl.when(inner_row)
+        def _():
+            for copy in x_full(k):
+                copy.start()
+
+        @pl.when(first)
+        def _():
+            for copy in x_first(k):
+                copy.start()
+            for copy in mirror(k):
+                copy.start()
+
+        @pl.when(last)
+        def _():
+            for copy in x_last(k):
+                copy.start()
+
     start_copy.wait()
     for copy in t_copies():
         copy.wait_recv()
@@ -369,6 +373,8 @@
             return jnp.where(lane < 64, upper, lower)
 
         cells = [jnp.concatenate([column[c, 4 + cycle, rows, :], edge(c)], 1) for c in range(6)]
+        old = [result[c, cycle, rows, :] for c in range(6)]
+        new = []
         material = jnp.concatenate([column_ph[4 + cycle, rows, :].astype(jnp.float32), edge(6)], 1)
         inverse, pressure = primitives(cells, material > 0.5)
         velocity = cells[2] * inverse
@@ -378,15 +384,15 @@
         for c in range(6):
             upward, downward = split_flux(cells, velocity, pressure, 2, c)
             change = line_divergence(upward, downward, 1)[:, :256] * scale
-            value = 0.75 * result[c, cycle, rows, :] + 0.25 * cells[c][:, :256] - change
+            value = 0.75 * old[c] + 0.25 * cells[c][:, :256] - change
             if c == 1:
                 value = value + source_scale * (cells[2] * velocity + pressure)[:, :256]
             if c == 2:
                 value = value - source_scale * (cells[1] * velocity)[:, :256]
-            result[c, cycle, rows, :] = value
+            new.append(value)
+        for c in range(6):
+            result[c, cycle, rows, :] = new[c]
         return 0
-
-    lax.fori_loop(0, 16, azimuthal, 0)
 
     row8 = lax.broadcasted_iota(jnp.int32, (8, 128), 0)
 
@@ -469,17 +475,22 @@
                 radius = (row * 4 + j).astype(jnp.float32) + 0.5
                 result[c, j, rows, lanes] = result[c, j, rows, lanes] - (weighted[j + 1] - weighted[j]) * (0.5 * quarter / radius)
 
+    def axial_step(n, _):
+        axial(n)
+        return 0
+
+    lax.fori_loop(0, 8, azimuthal, 0)
+    arrive_and_forward(0)
+    lax.fori_loop(8, 12, azimuthal, 0)
+    arrive_and_forward(1)
+    lax.fori_loop(12, 16, azimuthal, 0)
+    arrive_and_forward(2)
     for copy in z_copies():
         copy.wait_recv()
-    arrive_and_forward(0)
-
-    def axial_pair(n, _):
-        axial(2 * n)
-        axial(2 * n + 1)
-        arrive_and_forward(n + 1)
-        return 0
-
-    lax.fori_loop(0, 4, axial_pair, 0)
+    lax.fori_loop(0, 4, axial_step, 0)
+    arrive_and_forward(3)
+    lax.fori_loop(4, 8, axial_step, 0)
+    arrive_and_forward(4)
 
     @pl.when(last)
     def _():
@@ -487,12 +498,13 @@
             copy.wait()
 
     def radial_step(k, _):
-        @pl.when(k + 5 < 8)
-        def _():
-            arrive_and_forward(k + 5)
-
         y_arrive(k)
         radial(k)
+
+        @pl.when(jnp.logical_and(lax.rem(k, 2) == 1, k < 6))
+        def _():
+            arrive_and_forward(5 + k // 2)
+
         return 0
 
     lax.fori_loop(0, 8, radial_step, 0)
@@ -607,12 +619,12 @@
 def shards(state_start, state_section, phase, cutoff):
     f32, i32 = jnp.float32, jnp.int32
     table, table_t = fourier_tables()
-    anywhere = pl.BlockSpec(memory_space=pl.ANY)
+    anywhere = pl.BlockSpec(memory_space=pltpu.HBM)
     dma = pltpu.SemaphoreType.DMA
     return pl.pallas_call(
         kernel,
         out_shape=jax.ShapeDtypeStruct(state_start.shape, f32),
-        in_specs=[anywhere, anywhere, anywhere, pl.BlockSpec(memory_space=pltpu.SMEM), anywhere, anywhere],
+        in_specs=[anywhere] * 6,
         out_specs=anywhere,
         scratch_shapes=[
             pltpu.VMEM((6, 12, 32, 256), f32),
@@ -634,10 +646,11 @@
             pltpu.VMEM((4, 96, 2 * KMODES), f32),
             pltpu.VMEM((4, 96, 2 * KMODES), f32),
             pltpu.VMEM((4, 96, 2 * KMODES), f32),
+            pltpu.SMEM((4,), i32),
             dma((8,)),
             dma((8,)),
             dma((6,)),
-            dma((3,)),
+            dma((4,)),
             dma((16,)),
             dma((16,)),
             dma((16,)),
@@ -651,7 +664,7 @@
             dma((12,)),
             dma((4,)),
         ],
-        compiler_params=pltpu.CompilerParams(collective_id=0, has_side_effects=True, vmem_limit_bytes=40 * 1024 * 1024),
+        compiler_params=pltpu.CompilerParams(collective_id=0, has_side_effects=True, vmem_limit_bytes=67043328),
         name="jet_section",
     )(state_start, state_section, phase, cutoff, jnp.asarray(table), jnp.asarray(table_t))
 

time: 75.7 us -> 52.7 us (0.70)
  Pallas kernels: 68.6 us -> 50.5 us
  local copies, waits for them, and re-layouts: 6.79 us -> 2.09 us
    pallas_call x1, Pallas kernels: 68.6 us -> 50.5 us  [shards(): pl.pallas_call(kernel, out_shape=jax.ShapeDtypeStruct(state_start.shape,...]
    unnamed x13 -> x1, local copies, waits for them, and re-layouts: 6.79 us -> 2.09 us
where the time goes in v2:
time: 52.7 us; the launch traced here: 52.6 us
  Pallas kernels  50.5 us (96%)
  local copies, waits for them, and re-layouts  2.09 us (4%)
    pallas_call x1, Pallas kernels, shards(): pl.pallas_call(kernel, out_shape=jax.ShapeDtypeStruct(state_start.shape,...  50.5 us
    unnamed x1, local copies, waits for them, and re-layouts  2.09 us

profile of v2, /device:TPU:1, one launch (start us, length us, event | category | flops | bytes accessed | tf_op | source)
XLA Modules:
  0.0 52.6 jit_solution(4336567059371275493)
XLA Ops:
  0.0 50.5 %jet_section.1 = f32[6,4,32,256]{3,2,1,0:T(8,128)} custom-call(f32[6,4,32,256]{3,2,1,0:T(8,128)} %start_hbm.1, f32[6,4,32,256]{3,2,1,0:T(8,128)} %section_hbm.1, s32[4,32,256]{2,1,0:T(8,128)} %phase_hbm.1, s32[4]{0:T(128)} %cutoff_hbm.1, f32[1024,128]{1,0:T(8,128)} %constant.4.clone.table_hbm, f32[4,128,256]{2,1,0:T(8,128)} %constant.5.clone.table_t_hbm), custom_call_target="tpu_custom_call" | custom-call | tf_op jit(solution)/shard_map/jet_section/pallas_call | solution.py:624
  50.5 2.1 %copy.8 = f32[6,4,32,256]{3,2,1,0:T(8,128)} copy(f32[6,4,32,256]{3,2,1,0:T(8,128)} %jet_section.1) | data formatting | bytes 1572864

commit v3 on v2

--- a/solution.py
+++ b/solution.py
@@ -114,6 +114,8 @@
     half_far,
     half_total,
     half_peer,
+    relay,
+    relay_ph,
     cutoff_smem,
     load_sem,
     load_ph_sem,
@@ -124,6 +126,8 @@
     y_send,
     y_recv,
     m_send,
+    r_send,
+    r_recv,
     z_send,
     z_recv,
     t_send,
@@ -198,6 +202,7 @@
         {"theta": theta_up},
         {"theta": theta_down},
         {"theta": theta_far},
+        {"row": partner, "theta": theta_far},
         {"gz": gz_up},
         {"gz": gz_down},
     ):
@@ -273,6 +278,55 @@
     def forward(k):
         target = jnp.where(odd == 1, lax.rem(row + 6, 8), lax.rem(row + 2, 8))
         return carry(k, 9 - 9 * odd, 1 + 7 * odd, 3, y_send, y_recv, {"row": target})
+
+    def relay_copies(j, out):
+        rows = pl.ds((j // 2) * 8, 8)
+        column_rows, lanes = piece(j + 4)
+        if out:
+            return (
+                pltpu.make_async_remote_copy(
+                    src_ref=column.at[:, pl.ds(5, 3), column_rows, lanes],
+                    dst_ref=relay.at[:, :, rows, lanes],
+                    send_sem=x_send.at[j + 4],
+                    recv_sem=r_recv.at[j],
+                    device_id={"row": partner, "theta": theta_far},
+                    device_id_type=MESH,
+                ),
+                pltpu.make_async_remote_copy(
+                    src_ref=column_ph.at[pl.ds(5, 3), column_rows, lanes],
+                    dst_ref=relay_ph.at[:, rows, lanes],
+                    send_sem=x_send.at[j + 12],
+                    recv_sem=r_recv.at[j + 4],
+                    device_id={"row": partner, "theta": theta_far},
+                    device_id_type=MESH,
+                ),
+            )
+        return (
+            pltpu.make_async_remote_copy(
+                src_ref=relay.at[:, :, rows, lanes],
+                dst_ref=column.at[:, pl.ds(1, 3), column_rows, lanes],
+                send_sem=r_send.at[j],
+                recv_sem=x_recv.at[j + 4],
+                device_id={"theta": theta_far},
+                device_id_type=MESH,
+            ),
+            pltpu.make_async_remote_copy(
+                src_ref=relay_ph.at[:, rows, lanes],
+                dst_ref=column_ph.at[pl.ds(1, 3), column_rows, lanes],
+                send_sem=r_send.at[j + 4],
+                recv_sem=x_recv.at[j + 12],
+                device_id={"theta": theta_far},
+                device_id_type=MESH,
+            ),
+        )
+
+    def hand_over(j):
+        @pl.when(row == 1)
+        def _():
+            for copy in relay_copies(j, True):
+                copy.wait_recv()
+            for copy in relay_copies(j, False):
+                copy.start()
 
     forwards = jnp.logical_or(jnp.logical_and(odd == 0, row < 6), jnp.logical_and(odd == 1, row > 1))
 
@@ -326,28 +380,33 @@
             ),
         )
 
-    pl.semaphore_wait(barrier, 8)
+    pl.semaphore_wait(barrier, 9)
     for copy in t_copies():
         copy.start()
     for copy in z_copies():
         copy.start()
 
-    for k in range(8):
-
-        @pl.when(inner_row)
-        def _():
+    @pl.when(inner_row)
+    def _():
+        for k in range(8):
             for copy in x_full(k):
                 copy.start()
 
-        @pl.when(first)
-        def _():
+    @pl.when(first)
+    def _():
+        for k in range(8):
+            for copy in mirror(k):
+                copy.start()
+            if k < 4:
+                for copy in relay_copies(k, True):
+                    copy.start()
+        for k in range(4):
             for copy in x_first(k):
                 copy.start()
-            for copy in mirror(k):
-                copy.start()
-
-        @pl.when(last)
-        def _():
+
+    @pl.when(last)
+    def _():
+        for k in range(8):
             for copy in x_last(k):
                 copy.start()
 
@@ -416,20 +475,18 @@
             result[c, cycle, :, lanes] = result[c, cycle, :, lanes] - change
 
     def arrive_and_forward(k):
-        @pl.when(jnp.logical_and(row != 1, row != 6))
+        @pl.when(forwards)
         def _():
             for copy in carry(k, 4, 4, 4, x_send, x_recv, to_partner):
                 copy.wait_recv()
-
-        @pl.when(jnp.logical_or(row == 1, row == 6))
+            for copy in forward(k):
+                copy.start()
+
+    def x_arrive(k):
+        @pl.when(jnp.logical_not(forwards))
         def _():
             for copy in carry(k, 4, 4, 3, x_send, x_recv, to_partner):
                 copy.wait_recv()
-
-        @pl.when(forwards)
-        def _():
-            for copy in forward(k):
-                copy.start()
 
     def y_arrive(k):
         @pl.when(row != 7)
@@ -483,101 +540,129 @@
     arrive_and_forward(0)
     lax.fori_loop(8, 12, azimuthal, 0)
     arrive_and_forward(1)
+    hand_over(0)
     lax.fori_loop(12, 16, azimuthal, 0)
     arrive_and_forward(2)
+    hand_over(1)
     for copy in z_copies():
         copy.wait_recv()
     lax.fori_loop(0, 4, axial_step, 0)
     arrive_and_forward(3)
+    hand_over(2)
     lax.fori_loop(4, 8, axial_step, 0)
     arrive_and_forward(4)
+    hand_over(3)
 
     @pl.when(last)
     def _():
         for copy in rims():
             copy.wait()
 
-    def radial_step(k, _):
-        y_arrive(k)
-        radial(k)
-
-        @pl.when(jnp.logical_and(lax.rem(k, 2) == 1, k < 6))
-        def _():
-            arrive_and_forward(5 + k // 2)
-
-        return 0
-
-    lax.fori_loop(0, 8, radial_step, 0)
+    def tile(o):
+        return pl.ds(o * 8, 8) if isinstance(o, int) else pl.ds(pl.multiple_of(o * 8, 8), 8)
 
     def out_copy(o):
-        rows = pl.ds(o * 8, 8)
-        return pltpu.make_async_copy(result.at[:, :, rows, :], out_hbm.at[:, :, rows, :], out_sem.at[o])
-
-    @pl.when(first)
-    def _():
-        for copy in table_loads():
-            copy.wait()
-        mine = lax.rem(theta, 2) * 96
-        other = 96 - mine
-        pairs = ((0, {"theta": sibling}), (4, {"theta": theta_far}), (8, {"theta": sibling}))
-
-        def share(step, o, source, target):
-            base, where = pairs[step]
-            return pltpu.make_async_remote_copy(
-                src_ref=source,
-                dst_ref=target,
-                send_sem=f_send.at[base + o],
-                recv_sem=f_recv.at[base + o],
-                device_id=where,
-                device_id_type=MESH,
-            )
-
-        def step_one(o):
-            return share(0, o, part.at[o, pl.ds(pl.multiple_of(other, 8), 96)], half_got.at[o])
-
-        def step_two(o):
-            return share(1, o, half_sum.at[o], half_far.at[o])
-
-        def step_three(o):
-            return share(2, o, half_total.at[o], half_peer.at[o])
-
-        for o in range(4):
-            values = result[:, :, pl.ds(8 * o, 8), :].reshape(192, 256)
-            part[o] = jnp.dot(values, table[...], precision=lax.Precision.HIGHEST, preferred_element_type=jnp.float32)
-            step_one(o).start()
-        for o in range(4):
-            step_one(o).wait_recv()
-            half_sum[o] = part[o, pl.ds(pl.multiple_of(mine, 8), 96)] + half_got[o]
-            step_two(o).start()
-        for o in range(4):
-            step_two(o).wait_recv()
-            half_total[o] = half_sum[o] + half_far[o]
-            step_three(o).start()
+        return pltpu.make_async_copy(result.at[:, :, tile(o), :], out_hbm.at[:, :, tile(o), :], out_sem.at[o])
+
+    mine = pl.multiple_of(lax.rem(theta, 2) * 96, 8)
+    other = pl.multiple_of(96 - lax.rem(theta, 2) * 96, 8)
+
+    def share(step, o, source, target, where):
+        return pltpu.make_async_remote_copy(
+            src_ref=source,
+            dst_ref=target,
+            send_sem=f_send.at[4 * step + o],
+            recv_sem=f_recv.at[4 * step + o],
+            device_id={"theta": where},
+            device_id_type=MESH,
+        )
+
+    def step_one(o):
+        return share(0, o, part.at[o, pl.ds(other, 96)], half_got.at[o], sibling)
+
+    def step_two(o):
+        return share(1, o, half_sum.at[o], half_far.at[o], theta_far)
+
+    def step_three(o):
+        return share(2, o, half_total.at[o], half_peer.at[o], sibling)
+
+    def filter_one(o):
+        values = result[:, :, tile(o), :].reshape(192, 256)
+        part[o] = jnp.dot(values, table[...], precision=lax.Precision.HIGHEST, preferred_element_type=jnp.float32)
+        step_one(o).start()
+
+    def filter_two(o):
+        step_one(o).wait_recv()
+        half_sum[o] = part[o, pl.ds(mine, 96)] + half_got[o]
+        step_two(o).start()
+
+    def filter_three(o):
+        step_two(o).wait_recv()
+        half_total[o] = half_sum[o] + half_far[o]
+        step_three(o).start()
+
+    def filter_last(o, _):
         order = lax.broadcasted_iota(jnp.int32, (8, 128), 1)
         order = jnp.where(order < KMODES, order, order - KMODES)
         mode_scale = jnp.where(order == 0, 1.0 / NT, 2.0 / NT)
         weights = [jnp.where(order <= cutoff_smem[i], mode_scale, 0.0) for i in range(4)]
         weights = jnp.concatenate(weights * 3, 0)
-        even_core = mine == 0
-        for o in range(4):
-            step_three(o).wait_recv()
-            own = half_total[o] * weights
-            peer = half_peer[o] * weights
-            lower = jnp.where(even_core, own, peer)
-            upper = jnp.where(even_core, peer, own)
-            coefficients = jnp.concatenate([lower, upper], 0)
-            values = jnp.dot(coefficients, table_t[...], precision=lax.Precision.HIGHEST, preferred_element_type=jnp.float32)
-            result[:, :, pl.ds(8 * o, 8), :] = values.reshape(6, 4, 8, 256)
+        even_core = lax.rem(theta, 2) == 0
+        step_three(o).wait_recv()
+        own = half_total[o] * weights
+        peer = half_peer[o] * weights
+        lower = jnp.where(even_core, own, peer)
+        upper = jnp.where(even_core, peer, own)
+        coefficients = jnp.concatenate([lower, upper], 0)
+        values = jnp.dot(coefficients, table_t[...], precision=lax.Precision.HIGHEST, preferred_element_type=jnp.float32)
+        result[:, :, tile(o), :] = values.reshape(6, 4, 8, 256)
+        out_copy(o).start()
+        return 0
+
+    @pl.when(first)
+    def _():
+        for copy in table_loads():
+            copy.wait()
+
+    def radial_step(k, _):
+        x_arrive(k)
+        y_arrive(k)
+        radial(k)
+        o = k // 2
+        whole = lax.rem(k, 2) == 1
+
+        @pl.when(jnp.logical_and(whole, k < 6))
+        def _():
+            arrive_and_forward(5 + o)
+
+        @pl.when(jnp.logical_and(whole, first))
+        def _():
+            filter_one(o)
+
+            @pl.when(o > 0)
+            def _():
+                filter_two(o - 1)
+
+        @pl.when(jnp.logical_and(whole, jnp.logical_not(first)))
+        def _():
             out_copy(o).start()
+
+        return 0
+
+    lax.fori_loop(0, 8, radial_step, 0)
+
+    @pl.when(first)
+    def _():
+        filter_two(3)
+        for o in range(3):
+            filter_three(o)
+        lax.fori_loop(0, 3, filter_last, 0)
+        filter_three(3)
+        lax.fori_loop(3, 4, filter_last, 0)
         for o in range(4):
             step_one(o).wait_send()
             step_two(o).wait_send()
             step_three(o).wait_send()
-
-    @pl.when(jnp.logical_not(first))
-    def _():
-        for o in range(4):
-            out_copy(o).start()
 
     for copy in t_copies():
         copy.wait_send()
@@ -603,6 +688,12 @@
         @pl.when(forwards)
         def _():
             for copy in forward(k):
+                copy.wait_send()
+
+    @pl.when(row == 1)
+    def _():
+        for j in range(4):
+            for copy in relay_copies(j, False):
                 copy.wait_send()
 
     for o in range(4):
@@ -646,6 +737,8 @@
             pltpu.VMEM((4, 96, 2 * KMODES), f32),
             pltpu.VMEM((4, 96, 2 * KMODES), f32),
             pltpu.VMEM((4, 96, 2 * KMODES), f32),
+            pltpu.VMEM((6, 3, 16, 256), f32),
+            pltpu.VMEM((3, 16, 256), i32),
             pltpu.SMEM((4,), i32),
             dma((8,)),
             dma((8,)),
@@ -656,6 +749,8 @@
             dma((16,)),
             dma((16,)),
             dma((16,)),
+            dma((8,)),
+            dma((8,)),
             dma((4,)),
             dma((4,)),
             dma((2,)),

time: 52.7 us -> 43.1 us (0.82)
  Pallas kernels: 50.5 us -> 40.9 us
    pallas_call x1, Pallas kernels: 50.5 us -> 40.9 us  [shards(): pl.pallas_call(kernel, out_shape=jax.ShapeDtypeStruct(state_start.shape,...]
where the time goes in v3:
time: 43.1 us; the launch traced here: 43 us
  Pallas kernels  40.9 us (95%)
  local copies, waits for them, and re-layouts  2.09 us (5%)
    pallas_call x1, Pallas kernels, shards(): pl.pallas_call(kernel, out_shape=jax.ShapeDtypeStruct(state_start.shape,...  40.9 us
    unnamed x1, local copies, waits for them, and re-layouts  2.09 us

profile of v3, /device:TPU:1, one launch (start us, length us, event | category | flops | bytes accessed | tf_op | source)
XLA Modules:
  0.0 43.0 jit_solution(15222914702188965335)
XLA Ops:
  0.0 40.9 %jet_section.1 = f32[6,4,32,256]{3,2,1,0:T(8,128)} custom-call(f32[6,4,32,256]{3,2,1,0:T(8,128)} %start_hbm.1, f32[6,4,32,256]{3,2,1,0:T(8,128)} %section_hbm.1, s32[4,32,256]{2,1,0:T(8,128)} %phase_hbm.1, s32[4]{0:T(128)} %cutoff_hbm.1, f32[1024,128]{1,0:T(8,128)} %constant.4.clone.table_hbm, f32[4,128,256]{2,1,0:T(8,128)} %constant.5.clone.table_t_hbm), custom_call_target="tpu_custom_call" | custom-call | tf_op jit(solution)/shard_map/jet_section/pallas_call | solution.py:715
  40.9 2.1 %copy.8 = f32[6,4,32,256]{3,2,1,0:T(8,128)} copy(f32[6,4,32,256]{3,2,1,0:T(8,128)} %jet_section.1) | data formatting | bytes 1572864

commit v4 on v3

--- a/solution.py
+++ b/solution.py
@@ -11,7 +11,7 @@
 
 NT = 1024
 KMODES = 64
-GHOST = 3
+DIRECT = 3
 
 split_speed = 10.0
 time_step = 0.05
@@ -87,13 +87,22 @@
     return face - ahead(face, -1)
 
 
+def product(values, high_ref, low_ref):
+    high = values.astype(jnp.bfloat16)
+    low = (values - high.astype(jnp.float32)).astype(jnp.bfloat16)
+    dot = functools.partial(jnp.dot, preferred_element_type=jnp.float32)
+    return dot(high, high_ref[...]) + (dot(low, high_ref[...]) + dot(high, low_ref[...]))
+
+
 def kernel(
     start_hbm,
     section_hbm,
     phase_hbm,
     cutoff_hbm,
     table_hbm,
+    table_low_hbm,
     table_t_hbm,
+    table_t_low_hbm,
     out_hbm,
     column,
     column_ph,
@@ -107,7 +116,9 @@
     got_low,
     got_high,
     table,
+    table_low,
     table_t,
+    table_t_low,
     part,
     half_got,
     half_sum,
@@ -123,8 +134,11 @@
     misc_sem,
     x_send,
     x_recv,
+    b_send,
+    b_recv,
     y_send,
     y_recv,
+    c_recv,
     m_send,
     r_send,
     r_recv,
@@ -179,8 +193,10 @@
 
     def table_loads():
         return (
-            pltpu.make_async_copy(table_hbm.at[pl.ds(pl.multiple_of(theta * 256, 256), 256)], table, misc_sem.at[1]),
+            pltpu.make_async_copy(table_hbm.at[theta], table, misc_sem.at[1]),
             pltpu.make_async_copy(table_t_hbm.at[theta], table_t, misc_sem.at[2]),
+            pltpu.make_async_copy(table_low_hbm.at[theta], table_low, misc_sem.at[4]),
+            pltpu.make_async_copy(table_t_low_hbm.at[theta], table_t_low, misc_sem.at[5]),
             pltpu.make_async_copy(cutoff_hbm, cutoff_smem, misc_sem.at[3]),
         )
 
@@ -236,12 +252,11 @@
     lane = lax.broadcasted_iota(jnp.int32, (8, 128), 1)
 
     def pack(n, _):
-        pair = n // 4
-        rows = pl.ds(pl.multiple_of((n % 4) * 8, 8), 8)
+        rows = pl.ds(pl.multiple_of(n * 8, 8), 8)
         low = jnp.zeros((8, 128), jnp.float32)
         high = jnp.zeros((8, 128), jnp.float32)
-        for group in range(14):
-            channel, cycle = group % 7, 4 + 2 * pair + group // 7
+        for group in range(28):
+            channel, cycle = group % 7, 4 + group // 7
             if channel < 6:
                 near = column[channel, cycle, rows, pl.ds(0, 128)]
                 far = column[channel, cycle, rows, pl.ds(128, 128)]
@@ -249,28 +264,30 @@
                 near = column_ph[cycle, rows, pl.ds(0, 128)].astype(jnp.float32)
                 far = column_ph[cycle, rows, pl.ds(128, 128)].astype(jnp.float32)
             if group:
-                near = pltpu.roll(near, 8 * group, 1)
-            far = pltpu.roll(far, (8 * group + 8) % 128, 1)
-            here = lane // 8 == group
+                near = pltpu.roll(near, 4 * group, 1)
+            far = pltpu.roll(far, (4 * group + 4) % 128, 1)
+            here = lane // 4 == group
             low = jnp.where(here, near, low)
             high = jnp.where(here, far, high)
-        pack_low[pair, rows, :] = low
-        pack_high[pair, rows, :] = high
+        pack_low[rows, :] = low
+        pack_high[rows, :] = high
         return 0
 
-    lax.fori_loop(0, 8, pack, 0)
+    lax.fori_loop(0, 4, pack, 0)
 
     inner_row = jnp.logical_and(row > 0, row < 7)
     to_partner = {"row": partner}
 
-    def x_full(k):
-        return carry(k, 4, 8 * odd, 4, x_send, x_recv, to_partner)
+    swapped = jnp.logical_and(odd == 1, inner_row) & (row > 1)
+
+    def x_three(k):
+        return carry(k, jnp.where(swapped, 5, 4), jnp.where(swapped, 9, 8 * odd), 3, x_send, x_recv, to_partner)
+
+    def x_fourth(k):
+        return carry(k, jnp.where(swapped, 4, 7), jnp.where(swapped, 8, 3 + 8 * odd), 1, b_send, b_recv, to_partner)
 
     def x_first(k):
         return carry(k, 5, 1, 3, x_send, x_recv, to_partner)
-
-    def x_last(k):
-        return carry(k, 4, 8, 3, x_send, x_recv, to_partner)
 
     def mirror(k):
         return carry(k, 4, 1, 3, m_send, y_recv, {"theta": theta_far})
@@ -279,54 +296,66 @@
         target = jnp.where(odd == 1, lax.rem(row + 6, 8), lax.rem(row + 2, 8))
         return carry(k, 9 - 9 * odd, 1 + 7 * odd, 3, y_send, y_recv, {"row": target})
 
-    def relay_copies(j, out):
-        rows = pl.ds((j // 2) * 8, 8)
-        column_rows, lanes = piece(j + 4)
-        if out:
-            return (
-                pltpu.make_async_remote_copy(
-                    src_ref=column.at[:, pl.ds(5, 3), column_rows, lanes],
-                    dst_ref=relay.at[:, :, rows, lanes],
-                    send_sem=x_send.at[j + 4],
-                    recv_sem=r_recv.at[j],
-                    device_id={"row": partner, "theta": theta_far},
-                    device_id_type=MESH,
-                ),
-                pltpu.make_async_remote_copy(
-                    src_ref=column_ph.at[pl.ds(5, 3), column_rows, lanes],
-                    dst_ref=relay_ph.at[:, rows, lanes],
-                    send_sem=x_send.at[j + 12],
-                    recv_sem=r_recv.at[j + 4],
-                    device_id={"row": partner, "theta": theta_far},
-                    device_id_type=MESH,
-                ),
-            )
+    def forward_two(k):
+        return carry(k, 9, 1, 2, y_send, y_recv, {"row": 2})
+
+    def arrival(k, count, recv):
+        return carry(k, 4, 4, count, x_send, recv, to_partner)
+
+    def through(k, source, source_ph, target, target_ph, send, recv, where):
+        rows, lanes = piece(k)
         return (
             pltpu.make_async_remote_copy(
-                src_ref=relay.at[:, :, rows, lanes],
-                dst_ref=column.at[:, pl.ds(1, 3), column_rows, lanes],
-                send_sem=r_send.at[j],
-                recv_sem=x_recv.at[j + 4],
-                device_id={"theta": theta_far},
+                src_ref=source.at[:, :, rows, lanes],
+                dst_ref=target.at[:, :, rows, lanes],
+                send_sem=send.at[k],
+                recv_sem=recv.at[k],
+                device_id=where,
                 device_id_type=MESH,
             ),
             pltpu.make_async_remote_copy(
-                src_ref=relay_ph.at[:, rows, lanes],
-                dst_ref=column_ph.at[pl.ds(1, 3), column_rows, lanes],
-                send_sem=r_send.at[j + 4],
-                recv_sem=x_recv.at[j + 12],
-                device_id={"theta": theta_far},
+                src_ref=source_ph.at[:, rows, lanes],
+                dst_ref=target_ph.at[:, rows, lanes],
+                send_sem=send.at[k + 8],
+                recv_sem=recv.at[k + 8],
+                device_id=where,
                 device_id_type=MESH,
             ),
         )
 
-    def hand_over(j):
+    def planes_of(start, count):
+        return column.at[:, pl.ds(start, count)], column_ph.at[pl.ds(start, count)]
+
+    one_plane = relay.at[:, pl.ds(0, 1)], relay_ph.at[pl.ds(0, 1)]
+
+    def relay_out(k):
+        return through(k, *planes_of(5, 3), relay, relay_ph, x_send, r_recv, {"row": partner, "theta": theta_far})
+
+    def relay_on(k):
+        return through(k, relay, relay_ph, *planes_of(1, 3), r_send, x_recv, {"theta": theta_far})
+
+    def fourth_out(k):
+        return through(k, *planes_of(7, 1), *one_plane, b_send, r_recv, {"row": 3})
+
+    def fourth_on(k):
+        return through(k, *one_plane, *planes_of(3, 1), r_send, c_recv, {"row": 2})
+
+    def hand_over():
         @pl.when(row == 1)
         def _():
-            for copy in relay_copies(j, True):
-                copy.wait_recv()
-            for copy in relay_copies(j, False):
-                copy.start()
+            for k in range(DIRECT, 8):
+                for copy in relay_out(k):
+                    copy.wait_recv()
+                for copy in relay_on(k):
+                    copy.start()
+
+        @pl.when(row == 3)
+        def _():
+            for k in range(8):
+                for copy in fourth_out(k):
+                    copy.wait_recv()
+                for copy in fourth_on(k):
+                    copy.start()
 
     forwards = jnp.logical_or(jnp.logical_and(odd == 0, row < 6), jnp.logical_and(odd == 1, row > 1))
 
@@ -389,25 +418,37 @@
     @pl.when(inner_row)
     def _():
         for k in range(8):
-            for copy in x_full(k):
+            for copy in x_three(k):
                 copy.start()
+
+        @pl.when(row > 1)
+        def _():
+            for k in range(8):
+                for copy in x_fourth(k):
+                    copy.start()
+
+        @pl.when(row == 1)
+        def _():
+            for k in range(8):
+                for copy in fourth_out(k):
+                    copy.start()
 
     @pl.when(first)
     def _():
         for k in range(8):
             for copy in mirror(k):
                 copy.start()
-            if k < 4:
-                for copy in relay_copies(k, True):
+            if k >= DIRECT:
+                for copy in relay_out(k):
                     copy.start()
-        for k in range(4):
+        for k in range(DIRECT):
             for copy in x_first(k):
                 copy.start()
 
     @pl.when(last)
     def _():
         for k in range(8):
-            for copy in x_last(k):
+            for copy in x_three(k):
                 copy.start()
 
     start_copy.wait()
@@ -416,20 +457,20 @@
 
     quarter = 0.25 * time_step
 
+    lane16 = lax.broadcasted_iota(jnp.int32, (16, 128), 1)
+
     def azimuthal(n, _):
-        cycle = n // 4
-        octet = n % 4
-        rows = pl.ds(pl.multiple_of(octet * 8, 8), 8)
-        pair = cycle // 2
-        low = got_low[pair, rows, :]
-        high = got_high[pair, rows, :]
-        base = lax.rem(cycle, 2) * 56
+        cycle = n // 2
+        rows = pl.ds(pl.multiple_of((n % 2) * 16, 8), 16)
+        low = got_low[rows, :]
+        high = got_high[rows, :]
+        base = cycle * 28
 
         def edge(channel):
-            offset = base + 8 * channel
+            offset = base + 4 * channel
             upper = pltpu.roll(high, lax.rem(128 - offset, 128), 1)
-            lower = pltpu.roll(low, 120 - offset, 1)
-            return jnp.where(lane < 64, upper, lower)
+            lower = pltpu.roll(low, 124 - offset, 1)
+            return jnp.where(lane16 < 64, upper, lower)
 
         cells = [jnp.concatenate([column[c, 4 + cycle, rows, :], edge(c)], 1) for c in range(6)]
         old = [result[c, cycle, rows, :] for c in range(6)]
@@ -477,21 +518,39 @@
     def arrive_and_forward(k):
         @pl.when(forwards)
         def _():
-            for copy in carry(k, 4, 4, 4, x_send, x_recv, to_partner):
+            for copy in arrival(k, 3, x_recv):
                 copy.wait_recv()
+
+        @pl.when(jnp.logical_and(forwards, row > 0))
+        def _():
             for copy in forward(k):
                 copy.start()
 
+        @pl.when(first)
+        def _():
+            for copy in forward_two(k):
+                copy.start()
+
     def x_arrive(k):
         @pl.when(jnp.logical_not(forwards))
         def _():
-            for copy in carry(k, 4, 4, 3, x_send, x_recv, to_partner):
+            for copy in arrival(k, 3, x_recv):
                 copy.wait_recv()
 
+        @pl.when(jnp.logical_and(forwards, row > 0))
+        def _():
+            for copy in arrival(k, 1, b_recv):
+                copy.wait_recv()
+
     def y_arrive(k):
-        @pl.when(row != 7)
-        def _():
-            for copy in carry(k, 4, 4, 3, y_send, y_recv, to_partner):
+        @pl.when(jnp.logical_and(row != 7, row != 2))
+        def _():
+            for copy in arrival(k, 3, y_recv):
+                copy.wait_recv()
+
+        @pl.when(row == 2)
+        def _():
+            for copy in arrival(k, 2, y_recv) + arrival(k, 1, c_recv):
                 copy.wait_recv()
 
     flip = jnp.where(first, -1.0, 1.0)
@@ -536,22 +595,30 @@
         axial(n)
         return 0
 
-    lax.fori_loop(0, 8, azimuthal, 0)
-    arrive_and_forward(0)
-    lax.fori_loop(8, 12, azimuthal, 0)
-    arrive_and_forward(1)
-    hand_over(0)
-    lax.fori_loop(12, 16, azimuthal, 0)
-    arrive_and_forward(2)
-    hand_over(1)
+    def azimuthal_steps(n, _):
+        lax.fori_loop(2 * n, 2 * n + 2, azimuthal, 0)
+        arrive_and_forward(n)
+        return 0
+
+    lax.fori_loop(0, 4, azimuthal_steps, 0)
+    hand_over()
     for copy in z_copies():
         copy.wait_recv()
-    lax.fori_loop(0, 4, axial_step, 0)
-    arrive_and_forward(3)
-    hand_over(2)
-    lax.fori_loop(4, 8, axial_step, 0)
-    arrive_and_forward(4)
-    hand_over(3)
+
+    def axial_steps(n, _):
+        lax.fori_loop(2 * n, 2 * n + 2, axial_step, 0)
+
+        @pl.when(n < 3)
+        def _():
+            arrive_and_forward(4 + n)
+
+        return 0
+
+    lax.fori_loop(0, 4, axial_steps, 0)
+
+    @pl.when(row > 0)
+    def _():
+        arrive_and_forward(7)
 
     @pl.when(last)
     def _():
@@ -588,7 +655,7 @@
 
     def filter_one(o):
         values = result[:, :, tile(o), :].reshape(192, 256)
-        part[o] = jnp.dot(values, table[...], precision=lax.Precision.HIGHEST, preferred_element_type=jnp.float32)
+        part[o] = product(values, table, table_low)
         step_one(o).start()
 
     def filter_two(o):
@@ -614,7 +681,7 @@
         lower = jnp.where(even_core, own, peer)
         upper = jnp.where(even_core, peer, own)
         coefficients = jnp.concatenate([lower, upper], 0)
-        values = jnp.dot(coefficients, table_t[...], precision=lax.Precision.HIGHEST, preferred_element_type=jnp.float32)
+        values = product(coefficients, table_t, table_t_low)
         result[:, :, tile(o), :] = values.reshape(6, 4, 8, 256)
         out_copy(o).start()
         return 0
@@ -625,15 +692,15 @@
             copy.wait()
 
     def radial_step(k, _):
+        @pl.when(jnp.logical_and(first, k == 4))
+        def _():
+            arrive_and_forward(7)
+
         x_arrive(k)
         y_arrive(k)
         radial(k)
         o = k // 2
         whole = lax.rem(k, 2) == 1
-
-        @pl.when(jnp.logical_and(whole, k < 6))
-        def _():
-            arrive_and_forward(5 + o)
 
         @pl.when(jnp.logical_and(whole, first))
         def _():
@@ -669,31 +736,34 @@
     for copy in z_copies():
         copy.wait_send()
     for k in range(8):
+        for copy in x_first(k):
+            copy.wait_send()
 
         @pl.when(inner_row)
         def _():
-            for copy in x_full(k):
+            for copy in x_fourth(k):
                 copy.wait_send()
 
-        @pl.when(jnp.logical_not(inner_row))
-        def _():
-            for copy in x_last(k):
+        @pl.when(first)
+        def _():
+            for copy in mirror(k) + forward_two(k):
                 copy.wait_send()
 
-        @pl.when(first)
-        def _():
-            for copy in mirror(k):
-                copy.wait_send()
-
-        @pl.when(forwards)
+        @pl.when(jnp.logical_and(forwards, row > 0))
         def _():
             for copy in forward(k):
                 copy.wait_send()
 
     @pl.when(row == 1)
     def _():
-        for j in range(4):
-            for copy in relay_copies(j, False):
+        for k in range(DIRECT, 8):
+            for copy in relay_on(k):
+                copy.wait_send()
+
+    @pl.when(row == 3)
+    def _():
+        for k in range(8):
+            for copy in fourth_on(k):
                 copy.wait_send()
 
     for o in range(4):
@@ -703,19 +773,23 @@
 def fourier_tables():
     phases = (np.arange(NT)[:, None] * np.arange(KMODES)[None, :]) % NT
     angles = phases.astype(np.float64) * (2.0 * np.pi / NT)
-    table = np.concatenate([np.cos(angles), np.sin(angles)], 1).astype(np.float32)
-    return table, np.ascontiguousarray(table.reshape(4, 256, 2 * KMODES).transpose(0, 2, 1))
+    table = np.concatenate([np.cos(angles), np.sin(angles)], 1).astype(np.float32).reshape(4, 256, 2 * KMODES)
+    halves = []
+    for matrix in (table, np.ascontiguousarray(table.transpose(0, 2, 1))):
+        high = matrix.astype(jnp.bfloat16)
+        halves += [high, (matrix - high.astype(np.float32)).astype(jnp.bfloat16)]
+    return halves
 
 
 def shards(state_start, state_section, phase, cutoff):
     f32, i32 = jnp.float32, jnp.int32
-    table, table_t = fourier_tables()
+    tables = [jnp.asarray(matrix) for matrix in fourier_tables()]
     anywhere = pl.BlockSpec(memory_space=pltpu.HBM)
     dma = pltpu.SemaphoreType.DMA
     return pl.pallas_call(
         kernel,
         out_shape=jax.ShapeDtypeStruct(state_start.shape, f32),
-        in_specs=[anywhere] * 6,
+        in_specs=[anywhere] * 8,
         out_specs=anywhere,
         scratch_shapes=[
             pltpu.VMEM((6, 12, 32, 256), f32),
@@ -725,32 +799,28 @@
             pltpu.VMEM((4, 8, 256), i32),
             pltpu.VMEM((6, 4, 8, 256), f32),
             pltpu.VMEM((4, 8, 256), i32),
-            pltpu.VMEM((2, 32, 128), f32),
-            pltpu.VMEM((2, 32, 128), f32),
-            pltpu.VMEM((2, 32, 128), f32),
-            pltpu.VMEM((2, 32, 128), f32),
-            pltpu.VMEM((256, 2 * KMODES), f32),
-            pltpu.VMEM((2 * KMODES, 256), f32),
+            pltpu.VMEM((32, 128), f32),
+            pltpu.VMEM((32, 128), f32),
+            pltpu.VMEM((32, 128), f32),
+            pltpu.VMEM((32, 128), f32),
+            pltpu.VMEM((256, 2 * KMODES), jnp.bfloat16),
+            pltpu.VMEM((256, 2 * KMODES), jnp.bfloat16),
+            pltpu.VMEM((2 * KMODES, 256), jnp.bfloat16),
+            pltpu.VMEM((2 * KMODES, 256), jnp.bfloat16),
             pltpu.VMEM((4, 192, 2 * KMODES), f32),
             pltpu.VMEM((4, 96, 2 * KMODES), f32),
             pltpu.VMEM((4, 96, 2 * KMODES), f32),
             pltpu.VMEM((4, 96, 2 * KMODES), f32),
             pltpu.VMEM((4, 96, 2 * KMODES), f32),
             pltpu.VMEM((4, 96, 2 * KMODES), f32),
-            pltpu.VMEM((6, 3, 16, 256), f32),
-            pltpu.VMEM((3, 16, 256), i32),
+            pltpu.VMEM((6, 3, 32, 256), f32),
+            pltpu.VMEM((3, 32, 256), i32),
             pltpu.SMEM((4,), i32),
             dma((8,)),
             dma((8,)),
             dma((6,)),
-            dma((4,)),
-            dma((16,)),
-            dma((16,)),
-            dma((16,)),
-            dma((16,)),
-            dma((16,)),
-            dma((8,)),
-            dma((8,)),
+            dma((6,)),
+            *[dma((16,))] * 10,
             dma((4,)),
             dma((4,)),
             dma((2,)),
@@ -761,7 +831,7 @@
         ],
         compiler_params=pltpu.CompilerParams(collective_id=0, has_side_effects=True, vmem_limit_bytes=67043328),
         name="jet_section",
-    )(state_start, state_section, phase, cutoff, jnp.asarray(table), jnp.asarray(table_t))
+    )(state_start, state_section, phase, cutoff, *tables)
 
 
 def solution(mesh):

time: 43.1 us -> 40.9 us (0.949)
  Pallas kernels: 40.9 us -> 38.7 us
    pallas_call x1, Pallas kernels: 40.9 us -> 38.7 us  [shards(): pl.pallas_call(kernel, out_shape=jax.ShapeDtypeStruct(state_start.shape,...]
where the time goes in v4:
time: 40.9 us; the launch traced here: 40.8 us
  Pallas kernels  38.7 us (95%)
  local copies, waits for them, and re-layouts  2.09 us (5%)
    pallas_call x1, Pallas kernels, shards(): pl.pallas_call(kernel, out_shape=jax.ShapeDtypeStruct(state_start.shape,...  38.7 us
    unnamed x1, local copies, waits for them, and re-layouts  2.09 us

profile of v4, /device:TPU:1, one launch (start us, length us, event | category | flops | bytes accessed | tf_op | source)
XLA Modules:
  0.0 40.8 jit_solution(6751755924152259733)
XLA Ops:
  0.0 38.7 %jet_section.1 = f32[6,4,32,256]{3,2,1,0:T(8,128)} custom-call(f32[6,4,32,256]{3,2,1,0:T(8,128)} %start_hbm.1, f32[6,4,32,256]{3,2,1,0:T(8,128)} %section_hbm.1, s32[4,32,256]{2,1,0:T(8,128)} %phase_hbm.1, s32[4]{0:T(128)} %cutoff_hbm.1, bf16[4,256,128]{2,1,0:T(8,128)(2,1)} %constant.8.clone.table_hbm, bf16[4,256,128]{2,1,0:T(8,128)(2,1)} %constant.9.clone.table_low_hbm, ...), custom_call_target="tpu_custom_call" | custom-call | tf_op jit(solution)/shard_map/jet_section/pallas_call | solution.py:789
  38.7 2.1 %copy.10 = f32[6,4,32,256]{3,2,1,0:T(8,128)} copy(f32[6,4,32,256]{3,2,1,0:T(8,128)} %jet_section.1) | data formatting | bytes 1572864

commit v5 on v4

--- a/solution.py
+++ b/solution.py
@@ -12,6 +12,7 @@
 NT = 1024
 KMODES = 64
 DIRECT = 3
+ASIDE = 3
 
 split_speed = 10.0
 time_step = 0.05
@@ -299,6 +300,9 @@
     def forward_two(k):
         return carry(k, 9, 1, 2, y_send, y_recv, {"row": 2})
 
+    def forward_fourth(k):
+        return carry(k, 11, 3, 1, b_send, c_recv, {"row": 2})
+
     def arrival(k, count, recv):
         return carry(k, 4, 4, count, x_send, recv, to_partner)
 
@@ -351,7 +355,7 @@
 
         @pl.when(row == 3)
         def _():
-            for k in range(8):
+            for k in range(ASIDE, 8):
                 for copy in fourth_out(k):
                     copy.wait_recv()
                 for copy in fourth_on(k):
@@ -429,7 +433,10 @@
 
         @pl.when(row == 1)
         def _():
-            for k in range(8):
+            for k in range(ASIDE):
+                for copy in x_fourth(k):
+                    copy.start()
+            for k in range(ASIDE, 8):
                 for copy in fourth_out(k):
                     copy.start()
 
@@ -608,7 +615,7 @@
     def axial_steps(n, _):
         lax.fori_loop(2 * n, 2 * n + 2, axial_step, 0)
 
-        @pl.when(n < 3)
+        @pl.when(jnp.logical_and(row > 0, n < 3))
         def _():
             arrive_and_forward(4 + n)
 
@@ -619,6 +626,11 @@
     @pl.when(row > 0)
     def _():
         arrive_and_forward(7)
+
+    @pl.when(first)
+    def _():
+        arrive_and_forward(4)
+        arrive_and_forward(5)
 
     @pl.when(last)
     def _():
@@ -692,9 +704,20 @@
             copy.wait()
 
     def radial_step(k, _):
-        @pl.when(jnp.logical_and(first, k == 4))
+        @pl.when(jnp.logical_and(first, k == 2))
+        def _():
+            arrive_and_forward(6)
+
+        @pl.when(jnp.logical_and(first, k == 5))
         def _():
             arrive_and_forward(7)
+
+        @pl.when(jnp.logical_and(first, jnp.logical_and(k > 4, k < 5 + ASIDE)))
+        def _():
+            for copy in arrival(k - 5, 1, b_recv):
+                copy.wait_recv()
+            for copy in forward_fourth(k - 5):
+                copy.start()
 
         x_arrive(k)
         y_arrive(k)
@@ -723,9 +746,12 @@
         filter_two(3)
         for o in range(3):
             filter_three(o)
-        lax.fori_loop(0, 3, filter_last, 0)
+        lax.fori_loop(0, 2, filter_last, 0)
         filter_three(3)
-        lax.fori_loop(3, 4, filter_last, 0)
+        lax.fori_loop(2, 4, filter_last, 0)
+        for k in range(ASIDE):
+            for copy in forward_fourth(k):
+                copy.wait_send()
         for o in range(4):
             step_one(o).wait_send()
             step_two(o).wait_send()
@@ -762,7 +788,7 @@
 
     @pl.when(row == 3)
     def _():
-        for k in range(8):
+        for k in range(ASIDE, 8):
             for copy in fourth_on(k):
                 copy.wait_send()
 

time: 40.9 us -> 40.2 us (0.983)
  Pallas kernels: 38.7 us -> 37.9 us
    pallas_call x1, Pallas kernels: 38.7 us -> 37.9 us  [shards(): pl.pallas_call(kernel, out_shape=jax.ShapeDtypeStruct(state_start.shape,...]
where the time goes in v5:
time: 40.2 us; the launch traced here: 40 us
  Pallas kernels  37.9 us (94%)
  local copies, waits for them, and re-layouts  2.09 us (5%)
    pallas_call x1, Pallas kernels, shards(): pl.pallas_call(kernel, out_shape=jax.ShapeDtypeStruct(state_start.shape,...  37.9 us
    unnamed x1, local copies, waits for them, and re-layouts  2.09 us

profile of v5, /device:TPU:1, one launch (start us, length us, event | category | flops | bytes accessed | tf_op | source)
XLA Modules:
  0.0 40.0 jit_solution(6951409106517499105)
XLA Ops:
  0.0 37.9 %jet_section.1 = f32[6,4,32,256]{3,2,1,0:T(8,128)} custom-call(f32[6,4,32,256]{3,2,1,0:T(8,128)} %start_hbm.1, f32[6,4,32,256]{3,2,1,0:T(8,128)} %section_hbm.1, s32[4,32,256]{2,1,0:T(8,128)} %phase_hbm.1, s32[4]{0:T(128)} %cutoff_hbm.1, bf16[4,256,128]{2,1,0:T(8,128)(2,1)} %constant.8.clone.table_hbm, bf16[4,256,128]{2,1,0:T(8,128)(2,1)} %constant.9.clone.table_low_hbm, ...), custom_call_target="tpu_custom_call" | custom-call | tf_op jit(solution)/shard_map/jet_section/pallas_call | solution.py:815
  37.9 2.1 %copy.10 = f32[6,4,32,256]{3,2,1,0:T(8,128)} copy(f32[6,4,32,256]{3,2,1,0:T(8,128)} %jet_section.1) | data formatting | bytes 1572864

commit v6 on v5

--- a/solution.py
+++ b/solution.py
@@ -727,11 +727,11 @@
 
         @pl.when(jnp.logical_and(whole, first))
         def _():
-            filter_one(o)
-
             @pl.when(o > 0)
             def _():
                 filter_two(o - 1)
+
+            filter_one(o)
 
         @pl.when(jnp.logical_and(whole, jnp.logical_not(first)))
         def _():

time: 40.2 us -> 40.2 us (level)
  no operation moved by 1% of the time
where the time goes in v6:
time: 40.2 us; the launch traced here: 40 us
  Pallas kernels  37.9 us (94%)
  local copies, waits for them, and re-layouts  2.09 us (5%)
    pallas_call x1, Pallas kernels, shards(): pl.pallas_call(kernel, out_shape=jax.ShapeDtypeStruct(state_start.shape,...  37.9 us
    unnamed x1, local copies, waits for them, and re-layouts  2.09 us

profile of v6, /device:TPU:1, one launch (start us, length us, event | category | flops | bytes accessed | tf_op | source)
XLA Modules:
  0.0 40.0 jit_solution(4417959730771970551)
XLA Ops:
  0.0 37.9 %jet_section.1 = f32[6,4,32,256]{3,2,1,0:T(8,128)} custom-call(f32[6,4,32,256]{3,2,1,0:T(8,128)} %start_hbm.1, f32[6,4,32,256]{3,2,1,0:T(8,128)} %section_hbm.1, s32[4,32,256]{2,1,0:T(8,128)} %phase_hbm.1, s32[4]{0:T(128)} %cutoff_hbm.1, bf16[4,256,128]{2,1,0:T(8,128)(2,1)} %constant.8.clone.table_hbm, bf16[4,256,128]{2,1,0:T(8,128)(2,1)} %constant.9.clone.table_low_hbm, ...), custom_call_target="tpu_custom_call" | custom-call | tf_op jit(solution)/shard_map/jet_section/pallas_call | solution.py:815
  37.9 2.1 %copy.10 = f32[6,4,32,256]{3,2,1,0:T(8,128)} copy(f32[6,4,32,256]{3,2,1,0:T(8,128)} %jet_section.1) | data formatting | bytes 1572864
